TPU v7x, 32 devices: a whole 2x2x4 slice. The times are simulated.
32 devices in a mesh: wide: 8 (over z, x), narrow: 4 (over y, core).
Axes of the slice: x: 2, y: 2, z: 4, core: 2. Of those that a mesh axis runs over, the one named last changes fastest.
Arguments:
- rows: bfloat16 [8192, 1024], P(('wide', 'narrow')), may hold values from -6 to 6
- grades: int32 [8192], P(('wide', 'narrow')), may hold values from 0 to 4
- block_dest: int32 [32, 8], P(('wide', 'narrow')), may hold values from 0 to 7, each once within a row
- block_source: int32 [32, 8], P(('wide', 'narrow')), may hold values from 0 to 7, each once within a row
- lengths: int32 [8, 3], replicated, may hold values from 1 to 640, 1024 in all within a row
- gain: float32 [1024], replicated, may hold values from 0.5 to 1.5
- w_qkv: bfloat16 [1024, 3072], replicated, may hold values from -0.1875 to 0.1875
- w_out: bfloat16 [1024, 1024], replicated, may hold values from -0.1875 to 0.1875
- w_score: float32 [1024], replicated, may hold values from -0.1875 to 0.1875
Outputs:
- grad_rows: bfloat16 [8192, 1024], P(('wide', 'narrow'))
- grad_qkv: float32 [1024, 3072], P(None, ('wide', 'narrow'))
- grad_out: float32 [1024, 1024], P(None, ('wide', 'narrow'))
Inputs may be any that keep to these rules, and one draw needn't show every extreme that they name: Each row of block_dest and of block_source names every group once. The lengths of one group sum to 1024.
All inputs are finite; a program needn't handle non-finite values.
Results may differ from a plain program's by a relative error of at most 0.0095.
Values may be sent and summed in bfloat16 or wider, within the bound.
No kernel may reach another device: no remote copies, remote signals or barrier semaphores. Data moves between devices by JAX's collectives and lax.ppermute only.
A program may use at most 128 MiB of HBM per device.

v0:
```python
import jax
import jax.numpy as jnp
from jax import lax
from jax.experimental import pallas as pl
from jax.experimental.pallas import tpu as pltpu
from jax.sharding import PartitionSpec as P


HEADS = 16
LANES = 128
epsilon = 1e-06
loss_scale = 64.0
log2e = 1.4426950408889634
far = 2.0**100
bf16 = jnp.bfloat16
f32 = jnp.float32


def vmem():
    return pl.BlockSpec(memory_space=pltpu.VMEM)


def smem():
    return pl.BlockSpec(memory_space=pltpu.SMEM)


def whole(shape):
    return pl.BlockSpec(shape, lambda *_: (0,) * len(shape))


def call(kernel, shapes, specs, work=0, room=8, **more):
    params = pltpu.CompilerParams(vmem_limit_bytes=room * 2**20)
    cost = pl.CostEstimate(flops=work, transcendentals=0, bytes_accessed=0)
    return pl.pallas_call(
        kernel, out_shape=shapes, in_specs=specs, compiler_params=params, cost_estimate=cost, **more
    )


def indexed(kernel, shapes, specs, out_specs, grid, scratch=(), work=0, room=8):
    params = pltpu.CompilerParams(vmem_limit_bytes=room * 2**20)
    cost = pl.CostEstimate(flops=work, transcendentals=0, bytes_accessed=0)
    spec = pltpu.PrefetchScalarGridSpec(
        num_scalar_prefetch=1, grid=grid, in_specs=specs, out_specs=out_specs, scratch_shapes=scratch
    )
    return pl.pallas_call(
        kernel, out_shape=shapes, grid_spec=spec, compiler_params=params, cost_estimate=cost
    )


def near(values):
    return pltpu.with_memory_space_constraint(values, pltpu.VMEM)


def stay(values):
    return pltpu.with_memory_space_constraint(values, pltpu.HBM)


def contract(left, right, dims, **more):
    return lax.dot_general(left, right, (dims, ((), ())), preferred_element_type=f32, **more)


def prepare_kernel(w_v, w_out, score, u_out, turned_out, proj_out):
    width = w_v.shape[0]
    half = LANES // 2
    u = jnp.sum(w_out[...].astype(f32) * score[...], axis=1, keepdims=True)
    u_out[...] = u
    high = u.astype(bf16).astype(f32)
    lane = lax.broadcasted_iota(jnp.int32, (width, LANES), 1)
    head = lax.broadcasted_iota(jnp.int32, (width, LANES), 0) // (width // HEADS)
    columns = jnp.where(lane == head, high, 0.0)
    columns = jnp.where(lane == half + head, u - high, columns).astype(bf16)
    g = jnp.dot(w_v[...], columns, preferred_element_type=f32)
    g = g + pltpu.roll(g, half, axis=1)
    high = g.astype(bf16).astype(f32)
    tops, rests = high.T[:HEADS], (g - high).T[:HEADS]
    turned_out[...] = jnp.concatenate([tops, tops, rests], axis=0).astype(bf16)
    proj_out[...] = jnp.where(lane < half, high, g - high).astype(bf16)


def pack_kernel(dest, rows, grades, out):
    count, piece, width = rows.shape
    total = grades.shape[1]
    row = lax.broadcasted_iota(jnp.int32, (piece, total), 0)
    lane = lax.broadcasted_iota(jnp.int32, (piece, total), 1)
    line = grades[...].astype(f32)
    for b in range(count):
        grade = jnp.sum(jnp.where(lane == row + b * piece, line, 0.0), axis=1, keepdims=True)
        out[dest[0, b], :, :width] = rows[b]
        out[dest[0, b], :, width:] = jnp.broadcast_to(grade, (piece, LANES)).astype(bf16)


def norm_kernel(source, table, incoming, gain, score, ready, out, info_out, held):
    count, piece, wide = incoming.shape
    width = wide - LANES
    lane = lax.broadcasted_iota(jnp.int32, (piece, LANES), 1)
    for c in range(count):
        block = incoming[source[0, c]]
        values = block[:, :width].astype(f32)
        inverse = lax.rsqrt(jnp.mean(values * values, axis=1, keepdims=True) + epsilon)
        out[c] = (values * inverse * gain[...]).astype(bf16)
        base = jnp.sum(values * score[...], axis=1, keepdims=True)
        grades = block[:, width:].astype(f32)
        held[c * piece : (c + 1) * piece, :] = jnp.where(lane == 0, base, jnp.exp2(grades))
    info_out[...] = held[...].T[:8]


def list_of(table, narrow, lists, first, shape, axis):
    position = lax.broadcasted_iota(jnp.int32, shape, axis) + first
    found = jnp.zeros(shape, jnp.int32)
    for s in range(lists):
        found = found + (position >= table[narrow + s]).astype(jnp.int32)
    return found


def project(block, w_q, w_k, g):
    half = LANES // 2
    query = jnp.dot(block, w_q, preferred_element_type=f32) * half**-0.5
    key = jnp.dot(block, w_k, preferred_element_type=f32)
    turned = jnp.dot(block, g, preferred_element_type=f32).T
    return query.astype(bf16), key.astype(bf16), turned[:HEADS] + turned[half : half + HEADS]


def early_kernel(table, first, second, w_q, w_k, g, w_out, q_out, k_out, z_out):
    local = first.shape[0]
    own = w_q.shape[1]
    w_out[:, :own] = w_q[...]
    w_out[:, own:] = w_k[...]
    for m, block in enumerate((first, second)):
        rows = slice(m * local, (m + 1) * local)
        q_out[rows, :], k_out[rows, :], z_out[:, rows] = project(block[...], w_q[...], w_k[...], g[...])


def forward_kernel(table, *refs, narrow, lists):
    blocks, infos = refs[:narrow], refs[narrow : 2 * narrow]
    refs = refs[2 * narrow :]
    w, q_early, k_early, z_early, g, k_out, e_out, q_out, x_out, stat_out, part_out, z_out, lines_out = refs[:13]
    qs, kx, zt = refs[13:]
    local = blocks[0].shape[0]
    own = q_early.shape[1]
    heads = e_out.shape[0]
    half = LANES // 2
    step = pl.program_id(0)

    @pl.when(step == 0)
    def _():
        lane = lax.broadcasted_iota(jnp.int32, (local, LANES), 1)
        for m in range(narrow):
            rows = pl.ds(m * local, local)
            x_out[rows, :] = blocks[m][...]
            if m < 2:
                query, keys, turned = q_early[rows, :], k_early[rows, :], z_early[:, rows]
            else:
                query, keys, turned = project(blocks[m][...], w[:, :own], w[:, own:], g[...])
            qs[rows, :] = query
            k_out[rows, :] = keys
            zt[:, rows] = turned
            segment = list_of(table, narrow, lists, table[m] * local, (local, LANES), 0)
            away = jnp.where(lane == segment, 0.0, -far).astype(bf16)
            for p in range(heads // 2):
                kx[p, rows, :LANES] = keys[:, p * LANES : (p + 1) * LANES]
                kx[p, rows, LANES:] = away
            lines_out[:, rows] = infos[m][...]
            lines_out[2:3, rows] = list_of(table, narrow, lists, table[m] * local, (1, local), 1).astype(f32)
        z_out[...] = zt[...]

    at = pl.ds(pl.multiple_of(step * local, local), local)
    query = qs[at, :]
    q_out[...] = query
    lane = lax.broadcasted_iota(jnp.int32, (local, LANES), 1)
    segment = list_of(table, narrow, lists, table[step] * local, (local, LANES), 0)
    mine = (lane == segment).astype(f32).astype(bf16)
    stats = jnp.zeros((local, LANES), f32)
    zsum = jnp.zeros((local, 1), f32)
    for p in range(heads // 2):
        for s in range(2):
            h = 2 * p + s
            own = query[:, p * LANES : (p + 1) * LANES]
            own = jnp.where((lane >= half) == (s == 1), own, jnp.zeros_like(own))
            logits = contract(jnp.concatenate([own, mine], axis=1), kx[p], ((1,), (1,)))
            weights = jnp.exp2(logits * log2e)
            e_out[h] = weights.astype(bf16)
            zrow = zt[pl.ds(table[0] * heads + h, 1), :]
            inverse = 1.0 / jnp.sum(weights, axis=1, keepdims=True)
            zeta = jnp.sum(weights * zrow, axis=1, keepdims=True) * inverse
            stats = jnp.where(lane == h, zeta, stats)
            stats = jnp.where(lane == heads + h, inverse, stats)
            zsum = zsum + zeta
    stat_out[...] = stats
    part_out[...] = jnp.broadcast_to(zsum, (local, LANES)).T[:1]


def center_kernel(table, e, stat, key, z, a_out):
    heads = e.shape[0]
    rows = stat.shape[0]
    half = LANES // 2
    here = pl.ds(pl.multiple_of(pl.program_id(0) * rows, rows), rows)
    lane = lax.broadcasted_iota(jnp.int32, (rows, LANES), 1)
    stats = stat[...]
    for p in range(heads // 2):
        at = slice(p * LANES, (p + 1) * LANES)
        parts = []
        for h in (2 * p, 2 * p + 1):
            zrow = z[pl.ds(table[0] * heads + h, 1), :]
            centred = (e[h, here, :].astype(f32) * (zrow - stats[:, h : h + 1])).astype(bf16)
            part = jnp.dot(centred, key[:, at], preferred_element_type=f32)
            parts.append(part * stats[:, heads + h : heads + h + 1])
        a_out[:, at] = jnp.where(lane >= half, parts[1], parts[0]).astype(bf16)


def halves(blocks, pairs, wide_index, keep_out, send_out):
    odd = wide_index % 2 == 1
    for t in range(pairs):
        even, other = blocks(2 * t), blocks(2 * t + 1)
        place = jnp.bitwise_xor(t, wide_index // 2)
        keep_out[place] = jnp.where(odd, other, even).astype(bf16)
        send_out[place] = jnp.where(odd, even, other).astype(bf16)


def score_kernel(table, *refs, narrow, lists):
    partials = refs[:narrow]
    given, x, a, grad_out, keep_out, send_out, lines, acc = refs[narrow:]
    local, _ = a.shape
    width = x.shape[1]
    scale = (LANES // 2) ** -0.5
    pairs, _, chunk = keep_out.shape
    step = pl.program_id(0)

    @pl.when(step == 0)
    def _():
        acc[...] = jnp.zeros_like(acc)
        lines[...] = given[...]
        for m in range(narrow):
            rows = pl.ds(m * local, local)
            summed = given[0:1, rows]
            for d in range(narrow):
                summed = summed + partials[d][:, (m ^ d) * local : ((m ^ d) + 1) * local]
            lines[0:1, rows] = summed

    at = pl.ds(pl.multiple_of(step * local, local), local)
    turned = jnp.concatenate([lines[:, at]] * (LANES // 8), axis=0).T
    same = turned[:, 2:3] == lines[2:3, :]
    gains = lines[1:2, :]
    spread = gains - turned[:, 1:2]
    margin = turned[:, 0:1] - lines[0:1, :]
    margin = jnp.where(spread > 0.0, margin, -margin)
    pulls = spread / (1.0 + jnp.exp(-margin))
    pulls = jnp.sum(jnp.where(same, pulls, 0.0), axis=1, keepdims=True)
    norm = jnp.sum(jnp.where(same, gains, 0.0), axis=1, keepdims=True)
    grad = loss_scale * pulls / norm
    grad_out[...] = grad
    query = (a[...].astype(f32) * (grad * scale)).astype(bf16)
    acc[...] += contract(query, x[:, :width], ((0,), (0,)))

    @pl.when(step == pl.num_programs(0) - 1)
    def _():
        cut = lambda w: acc[:, w * chunk : (w + 1) * chunk]
        halves(cut, pairs, table[narrow + lists], keep_out, send_out)


def key_kernel(table, e, stat, query, z, grad, w_v, x_hbm, keys_out, keep_out, send_out, x, key_acc, c_acc, sem, at_wide):
    heads, total, _ = e.shape
    rows = query.shape[0]
    half = LANES // 2
    own = query.shape[1]
    width = w_v.shape[0]
    pairs, lines, chunk = keep_out.shape
    step = pl.program_id(0)
    copy = pltpu.make_async_copy(x_hbm, x, sem)

    @pl.when(step == 0)
    def _():
        copy.start()
        key_acc[...] = jnp.zeros_like(key_acc)
        c_acc[...] = jnp.zeros_like(c_acc)

    lane = lax.broadcasted_iota(jnp.int32, (rows, LANES), 1)
    stats = stat[...]
    here = pl.ds(pl.multiple_of(step * rows, rows), rows)
    for h in range(heads):
        p, s = h // 2, h % 2
        zeta = stats[:, h : h + 1]
        scaled = e[h, here, :].astype(f32) * (stats[:, heads + h : heads + h + 1] * grad[...])
        c_acc[h : h + 1, :] += jnp.sum(scaled, axis=0, keepdims=True)
        centred = (scaled * (z[pl.ds(table[0] * heads + h, 1), :] - zeta)).astype(bf16)
        head = query[:, p * LANES : (p + 1) * LANES]
        head = jnp.where((lane >= half) == (s == 1), head, jnp.zeros_like(head))
        key_acc[p * LANES : (p + 1) * LANES, :] += contract(head, centred, ((0,), (0,)))

    @pl.when(step == pl.num_programs(0) - 1)
    def _():
        copy.wait()
        c = c_acc[...]
        high = c.astype(bf16).astype(f32)
        parts = jnp.concatenate([high[:heads], (c - high)[:heads]], axis=0)
        extra = keys_out.shape[0] - own - 2 * heads
        parts = jnp.concatenate([parts, jnp.zeros((extra, total), f32)], axis=0)
        keys_out[:own] = key_acc[...].astype(bf16)
        keys_out[own:] = parts.astype(bf16)
        out = jnp.dot(keys_out[...], x[:, :width], preferred_element_type=f32)
        mass = out[own : own + heads] + out[own + heads : own + 2 * heads]
        high = mass.astype(bf16).astype(f32)
        tops = jnp.concatenate([high, mass - high], axis=0)
        values = jnp.dot(tops.astype(bf16), w_v[...], preferred_element_type=f32)
        values = values[:heads] + values[heads:]
        head = lax.broadcasted_iota(jnp.int32, (heads, own), 1) // half
        index = lax.broadcasted_iota(jnp.int32, (heads, own), 0)
        value = jnp.sum(jnp.where(head == index, values, 0.0), axis=0, keepdims=True)
        count = own // chunk
        cuts = [value[:, t * chunk : (t + 1) * chunk] for t in range(count)]
        fill = lines - own - heads - count
        cuts.append(jnp.zeros((fill, chunk), f32))

        def block(w):
            at = slice(w * chunk, (w + 1) * chunk)
            return jnp.concatenate([out[:own, at], mass[:, at]] + cuts, axis=0)

        halves(block, pairs, table[at_wide], keep_out, send_out)


def fetch(table, w, buffer, sems, first):
    narrow, _, own = buffer.shape
    copies = []
    for m in range(narrow):
        at = pl.ds(pl.multiple_of((table[m] + first) * own, own), own)
        copies.append(pltpu.make_async_copy(w.at[:, at], buffer.at[m], sems.at[m]))
        copies[m].start()
    return copies


def query_rows_kernel(table, *refs):
    *blocks, w, out, buffer, sems = refs
    copies = fetch(table, w, buffer, sems, 0)
    for m, block in enumerate(blocks):
        copies[m].wait()
        term = contract(block[...], buffer[m], ((1,), (1,)))
        out[...] = term if m == 0 else out[...] + term


def tail_kernel(table, *refs, narrow, heads):
    keys = refs[:narrow]
    w, query_rows, turned, source, incoming, grad, gain, score, out, acc, cs, buffer, sems = refs[narrow:]
    copies = fetch(table, w, buffer, sems, narrow)
    count, piece, width = out.shape
    own = width // narrow
    scale = (LANES // 2) ** -0.5
    acc[...] = query_rows[...] * (grad[...] * scale)
    for m in range(narrow):
        copies[m].wait()
        acc[...] += contract(keys[m][:own], buffer[m], ((0,), (1,)))
        mass = keys[m][own:].astype(f32)
        for h in range(heads):
            cs[pl.ds(table[m] * heads + h, 1), :] = mass[h : h + 1] + mass[heads + h : heads + h + 1]
    mass = cs[...]
    high = mass.astype(bf16).astype(f32)
    mass = jnp.concatenate([high, mass - high, high], axis=0).astype(bf16)
    acc[...] += contract(mass, turned[...], ((0,), (0,)))
    for c in range(count):
        part = pl.ds(c * piece, piece)
        scaled = acc[part, :] * gain[...]
        values = incoming[source[0, c], :, :width].astype(f32)
        inv = lax.rsqrt(jnp.mean(values * values, axis=1, keepdims=True) + epsilon)
        mean = jnp.mean(scaled * values, axis=1, keepdims=True)
        sums = grad[part, :] * score[...] + inv * scaled - values * (inv * inv * inv * mean)
        out[source[0, c]] = sums.astype(bf16)


def body(rows, grades, block_dest, block_source, lengths, gain, w_qkv, w_out, w_score):
    wide = lax.axis_size("wide")
    narrow = lax.axis_size("narrow")
    wide_index = lax.axis_index("wide")
    narrow_index = lax.axis_index("narrow")
    local, width = rows.shape
    lists = lengths.shape[1]
    piece = local // wide
    head_size = width // HEADS
    heads = HEADS // narrow
    own = heads * head_size
    total = local * narrow
    chunk = width // wide
    order = jnp.bitwise_xor(narrow_index, jnp.arange(narrow, dtype=jnp.int32))
    bounds = jnp.cumsum(lax.dynamic_index_in_dim(lengths, wide_index, 0, keepdims=False))
    table = jnp.concatenate([order, bounds.astype(jnp.int32), wide_index[None].astype(jnp.int32)])
    gain_row, score_row = gain[None, :], w_score[None, :]

    def swap(values, m):
        return lax.ppermute(values, "narrow", [(i, i ^ m) for i in range(narrow)])

    def across(values):
        return lax.all_to_all(values, "wide", split_axis=0, concat_axis=0, tiled=True)

    def spread(values):
        held = [values]
        for m in range(1, narrow):
            top = 1 << (m.bit_length() - 1)
            near_by = m ^ top
            held.append(swap(values, m) if near_by == 0 else None)
        for m in range(1, narrow):
            if held[m] is None:
                top = 1 << (m.bit_length() - 1)
                held[m] = swap(held[top], m ^ top)
        return held

    def shape(*dims, dtype=f32):
        return jax.ShapeDtypeStruct(dims, dtype)

    outgoing = call(
        pack_kernel, shape(wide, piece, width + LANES, dtype=bf16), [smem(), vmem(), vmem()]
    )(stay(block_dest), stay(rows.reshape(wide, piece, width)), stay(grades[None, :]))
    incoming = across(outgoing)

    u, g_turned, g_proj = call(
        prepare_kernel,
        (shape(width, 1), shape(3 * HEADS, width, dtype=bf16), shape(width, LANES, dtype=bf16)),
        [pl.BlockSpec((width, width), lambda i: (0, 2)), whole((width, width)), whole((1, width))],
        work=10**9,
        room=24,
        grid=(1,),
        out_specs=(whole((width, 1)), whole((3 * HEADS, width)), whole((width, LANES))),
    )(stay(w_qkv), w_out, score_row)

    normed, info = call(
        norm_kernel,
        (shape(wide, piece, width, dtype=bf16), shape(8, local)),
        [smem(), smem(), vmem(), vmem(), vmem(), pl.BlockSpec(memory_space=pl.ANY)],
        scratch_shapes=[pltpu.VMEM((local, LANES), f32)],
    )(block_source, table[None, :], near(incoming), gain_row, score_row, g_proj)
    blocks = spread(normed.reshape(local, width))
    infos = [info] + [swap(info, m) for m in range(1, narrow)]

    row_block = lambda columns: pl.BlockSpec((local, columns), lambda i, t: (i, 0))
    early = indexed(
        early_kernel,
        (
            shape(width, 2 * own, dtype=bf16),
            shape(2 * local, own, dtype=bf16),
            shape(2 * local, own, dtype=bf16),
            shape(HEADS, 2 * local),
        ),
        [
            vmem(),
            vmem(),
            pl.BlockSpec((width, own), lambda i, t: (0, t[0])),
            pl.BlockSpec((width, own), lambda i, t: (0, narrow + t[0])),
            vmem(),
        ],
        (vmem(),) * 4,
        (1,),
        work=10**9,
        room=10,
    )(table, near(blocks[0]), near(blocks[1]), stay(w_qkv), stay(w_qkv), near(g_proj))
    key, e, queries, x, stat, part, z, lines = indexed(
        lambda *refs: forward_kernel(*refs, narrow=narrow, lists=lists),
        (
            shape(total, own, dtype=bf16),
            shape(heads, total, total, dtype=bf16),
            shape(total, own, dtype=bf16),
            shape(total, width, dtype=bf16),
            shape(total, LANES),
            shape(1, total),
            shape(HEADS, total),
            shape(8, total),
        ),
        [vmem()] * (2 * narrow + 5),
        (
            whole((total, own)),
            pl.BlockSpec((heads, local, total), lambda i, t: (0, i, 0)),
            row_block(own),
            vmem(),
            row_block(LANES),
            pl.BlockSpec((1, local), lambda i, t: (0, i)),
            whole((HEADS, total)),
            whole((8, total)),
        ),
        (narrow,),
        [
            pltpu.VMEM((total, own), bf16),
            pltpu.VMEM((heads // 2, total, 2 * LANES), bf16),
            pltpu.VMEM((HEADS, total), f32),
        ],
        work=4 * 10**9,
        room=28,
    )(table, *map(near, [*blocks, *infos, *early, g_proj]))

    partials = [part] + [swap(part, m) for m in range(1, narrow)]
    a = indexed(
        center_kernel,
        shape(total, own, dtype=bf16),
        [vmem(), row_block(LANES), whole((total, own)), whole((HEADS, total))],
        row_block(own),
        (narrow,),
        work=2 * 10**9,
        room=10,
    )(table, near(e), stat, key, z)
    a_rows = [a[:local]] + [swap(a[m * local : (m + 1) * local], m) for m in range(1, narrow)]

    grad, keep_q, send_q = indexed(
        lambda *refs: score_kernel(*refs, narrow=narrow, lists=lists),
        (shape(total, 1),) + (shape(wide // 2, own, chunk, dtype=bf16),) * 2,
        [whole((1, total))] + [vmem()] * (narrow - 1) + [whole((8, total)), row_block(width), row_block(own)],
        (row_block(1),) + (whole((wide // 2, own, chunk)),) * 2,
        (narrow,),
        [pltpu.VMEM((8, total), f32), pltpu.VMEM((own, width), f32)],
        work=2 * 10**9,
        room=14,
    )(table, partials[0], *map(near, partials[1:]), lines, x, a)

    def to_partner(values, step):
        return lax.ppermute(values, "wide", [(i, i ^ step) for i in range(wide)])

    def added(kept, received):
        return kept.astype(f32) + received.astype(f32)

    got_q = to_partner(send_q, 1)

    count_v = own // chunk
    lines_k = -(-(own + heads + count_v) // 16) * 16
    lines_c = -(-(own + 2 * heads) // 16) * 16
    keys, keep, send = indexed(
        lambda *refs: key_kernel(*refs, at_wide=narrow + lists),
        (shape(lines_c, total, dtype=bf16),) + (shape(wide // 2, lines_k, chunk, dtype=bf16),) * 2,
        [
            vmem(),
            row_block(LANES),
            row_block(own),
            whole((HEADS, total)),
            row_block(1),
            pl.BlockSpec((width, own), lambda i, t: (0, 2 * narrow + t[0])),
            pl.BlockSpec(memory_space=pl.ANY),
        ],
        (whole((lines_c, total)),) + (whole((wide // 2, lines_k, chunk)),) * 2,
        (narrow,),
        [
            pltpu.VMEM((total, width), bf16),
            pltpu.VMEM((own, total), f32),
            pltpu.VMEM((8, total), f32),
            pltpu.SemaphoreType.DMA,
        ],
        work=4 * 10**9,
        room=22,
    )(table, near(e), stat, queries, z, grad, stay(w_qkv), x)

    k_rows = [keys[:, :local]]
    k_rows += [swap(keys[:, m * local : (m + 1) * local], m) for m in range(1, narrow)]
    got_k = to_partner(send, 1)
    sums = jnp.concatenate([added(keep_q, got_q), added(keep, got_k)], axis=1)
    step = 2
    while step < wide:
        cut = sums.astype(bf16).reshape(-1, 2, own + lines_k, chunk)
        sums = added(cut[:, 0], to_partner(cut[:, 1], step))
        step *= 2
    sums = sums[0].astype(bf16)

    fetched = [pltpu.VMEM((narrow, width, own), bf16), pltpu.SemaphoreType.DMA((narrow,))]
    anywhere = pl.BlockSpec(memory_space=pl.ANY)
    query_rows = indexed(
        query_rows_kernel,
        shape(local, width),
        [vmem()] * narrow + [anywhere],
        vmem(),
        (),
        fetched,
        work=10**9,
    )(table, *map(near, a_rows), stay(w_qkv))
    returning = indexed(
        lambda *refs: tail_kernel(*refs, narrow=narrow, heads=heads),
        shape(wide, piece, width, dtype=bf16),
        [vmem()] * narrow + [anywhere] + [vmem()] * 2 + [smem()] + [vmem()] * 4,
        vmem(),
        (),
        [pltpu.VMEM((local, width), f32), pltpu.VMEM((HEADS, local), f32)] + fetched,
        work=10**9,
        room=10,
    )(
        table, *map(near, k_rows), stay(w_qkv), near(query_rows), g_turned, block_source,
        near(incoming), grad[:local], gain_row, score_row,
    )
    arrived = across(returning)
    grad_rows = arrived[block_dest[0]].reshape(local, width)

    gathered = jnp.stack(spread(sums))[order]
    q_cols = gathered[:, :own].reshape(width, chunk)
    gathered = gathered[:, own:]
    k_cols = gathered[:, :own].reshape(width, chunk)
    m_all = gathered[:, own : own + heads].astype(f32)
    m_rows = jnp.broadcast_to(m_all.reshape(HEADS, 1, chunk), (HEADS, head_size, chunk))
    v_cols = (m_rows.reshape(width, chunk) * u).astype(bf16)
    v_all = gathered[:, own + heads : own + heads + count_v].astype(f32)
    v_all = v_all.reshape(width)
    columns = 3 * width // (wide * narrow)
    full = jnp.concatenate([q_cols, k_cols, v_cols], axis=0).reshape(wide, narrow, columns, chunk)
    mine = lax.dynamic_index_in_dim(full, narrow_index, 1, keepdims=False)
    parts = across(mine)
    grad_qkv = parts.astype(f32).transpose(0, 2, 1).reshape(width, columns)
    out_columns = width // (wide * narrow)
    place = (wide_index * narrow + narrow_index) * out_columns
    grad_out = v_all[:, None] * lax.dynamic_slice_in_dim(w_score, place, out_columns)[None, :]
    return (grad_rows, grad_qkv, grad_out)


def solution(mesh):
    both = ("wide", "narrow")
    placed = (P(both, None), P(both), P(both, None), P(both, None), P(), P(), P(), P(), P())
    return jax.shard_map(
        body,
        mesh=mesh,
        in_specs=placed,
        out_specs=(P(both, None), P(None, both), P(None, both)),
        check_vma=False,
    )
```

profile of v0, /device:TPU:0, one launch (start us, length us, event | category | flops | bytes accessed | tf_op | source)
XLA Modules:
  0.0 142.7 jit_solution(3725938559486395235)
XLA Ops:
  0.6 0.0 copy-start
  0.7 2.1 %shard_map.112 = bf16[8,32,1152]{2,1,0:T(8,128)(2,1)} custom-call(s32[1,8]{1,0:T(1,128)} %dest.1, bf16[8,32,1024]{2,1,0:T(8,128)(2,1)} %bitcast.78, s32[1,256]{1,0:T(1,128)} %bitcast.85), custom_call_target="tpu_custom_call" | custom-call | tf_op jit(solution)/shard_map/pallas_call | solution.py:406
  2.8 7.3 %all-to-all-start = ((bf16[8,32,1152]{2,1,0:T(8,128)(2,1)}), bf16[8,32,1152]{2,1,0:T(8,128)(2,1)S(1)}, u32[]{:S(2)}, u32[]{:S(2)}) async-start(bf16[8,32,1152]{2,1,0:T(8,128)(2,1)} %shard_map.112), calls=%async_computation | async-start | bytes 1179648 | tf_op jit(solution)/shard_map/all_to_all | solution.py:389
  10.1 0.2 dynamic-slice_reduce_fusion
  10.3 0.2 reduce-window.9
  10.5 0.0 copy-start.6
  10.5 2.9 %shard_map.113 = (f32[1024,1]{1,0:T(8,128)S(1)}, bf16[48,1024]{1,0:T(8,128)(2,1)S(1)}, bf16[1024,128]{1,0:T(8,128)(2,1)S(1)}) custom-call(bf16[1024,3072]{1,0:T(8,128)(2,1)} %refs_5_.1, bf16[1024,1024]{1,0:T(8,128)(2,1)S(1)} %copy-done.1, f32[1,1024]{1,0:T(1,128)S(1)} %bitcast.63), custom_call_target="tpu_custom_call" | custom-call | flops 1000000000 | tf_op jit(solution)/shard_map/pallas_call | solution.py:411
  13.4 0.7 copy-done.2
  14.0 0.1 pad_add_fusion.table.refs_0_
  14.1 11.9 %all-to-all-done.incoming.refs_9_ = bf16[8,32,1152]{2,1,0:T(8,128)(2,1)S(1)} async-done(((bf16[8,32,1152]{2,1,0:T(8,128)(2,1)}), bf16[8,32,1152]{2,1,0:T(8,128)(2,1)S(1)}, u32[]{:S(2)}, u32[]{:S(2)}) %all-to-all-start) | async-done | bytes 589856 | tf_op jit(solution)/shard_map/all_to_all | solution.py:389
  26.0 0.9 shard_map.114
  26.8 1.6 %collective-permute-start.1 = (bf16[256,1024]{1,0:T(8,128)(2,1)S(1)}, bf16[256,1024]{1,0:T(8,128)(2,1)S(1)}, u32[]{:S(2)}, u32[]{:S(2)}) collective-permute-start(bf16[256,1024]{1,0:T(8,128)(2,1)S(1)} %bitcast.59), channel_id=1, source_target_pairs={{0,2},{1,3},{2,0},{3,1},{4,6},{5,7},{6,4},{7,5},{8,10},{9,11},{10,... | collective-permute-start | bytes 1572872 | tf_op jit(solution)/shard_map/ppermute | solution.py:386
  28.4 10.7 %collective-permute-done.1.refs_3_ = bf16[256,1024]{1,0:T(8,128)(2,1)S(1)} collective-permute-done((bf16[256,1024]{1,0:T(8,128)(2,1)S(1)}, bf16[256,1024]{1,0:T(8,128)(2,1)S(1)}, u32[]{:S(2)}, u32[]{:S(2)}) %collective-permute-start.1) | collective-permute-done | bytes 524320 | tf_op jit(solution)/shard_map/ppermute | solution.py:386
  39.1 0.0 collective-permute-start.2
  39.1 1.6 %collective-permute-start.5 = (f32[8,256]{1,0:T(8,128)S(1)}, f32[8,256]{1,0:T(8,128)S(1)}, u32[]{:S(2)}, u32[]{:S(2)}) collective-permute-start(f32[8,256]{1,0:T(8,128)S(1)} %get-tuple-element.28.refs_5_), channel_id=1, source_target_pairs={{0,3},{1,2},{2,1},{3,0},{4,7},{5,6},{6,5},{7,4},{8,11},{9,10},{10,... | collective-permute-start | bytes 24584 | tf_op jit(solution)/shard_map/ppermute | solution.py:386
  40.8 0.5 collective-permute-start.4
  41.3 2.8 %shard_map.115 = (bf16[1024,512]{1,0:T(8,128)(2,1)S(1)}, bf16[512,256]{1,0:T(8,128)(2,1)S(1)}, bf16[512,256]{1,0:T(8,128)(2,1)S(1)}, f32[16,512]{1,0:T(8,128)S(1)}) custom-call(s32[8]{0:T(128)S(1)} %pad_add_fusion.table.refs_0_, bf16[256,1024]{1,0:T(8,128)(2,1)S(1)} %bitcast.61, bf16[256,1024]{1,0:T(8,128)(2,1)S(1)} %collective-permute-done.second.refs_2_, ...), custom_call_target="tpu_custom_call" | custom-call | flops 1000000000 | tf_op jit(solution)/shard_map/pallas_call | solution.py:431
  44.1 0.0 collective-permute-done.5.refs_8_
  44.1 0.3 collective-permute-done.4.refs_7_
  44.4 0.0 collective-permute-done.3.refs_6_
  44.4 7.5 %shard_map.116 = (bf16[1024,256]{1,0:T(8,128)(2,1)S(1)}, bf16[4,1024,1024]{2,1,0:T(8,128)(2,1)S(1)}, bf16[1024,256]{1,0:T(8,128)(2,1)S(1)}, bf16[1024,1024]{1,0:...) custom-call(s32[8]{0:T(128)S(1)} %pad_add_fusion.table.refs_0_, ...), custom_call_target="tpu_custom_call" | custom-call | flops 4000000000 | tf_op jit(solution)/shard_map/pallas_call | solution.py:451
  51.9 1.5 %collective-permute-start.8 = (f32[1,1024]{1,0:T(1,128)S(1)}, f32[1,1024]{1,0:T(1,128)S(1)}, u32[]{:S(2)}, u32[]{:S(2)}) collective-permute-start(f32[1,1024]{1,0:T(1,128)S(1)} %get-tuple-element.37.refs_1_), channel_id=1, source_target_pairs={{0,3},{1,2},{2,1},{3,0},{4,7},{5,6},{6,5},{7,4},{8,11},{9,10},{10,... | collective-permute-start | bytes 12296 | tf_op jit(solution)/shard_map/ppermute | solution.py:386
  53.4 0.5 collective-permute-start.7
  53.9 4.2 %shard_map.117.refs_7_ = bf16[1024,256]{1,0:T(8,128)(2,1)S(1)} custom-call(s32[8]{0:T(128)S(1)} %pad_add_fusion.table.refs_0_, bf16[4,1024,1024]{2,1,0:T(8,128)(2,1)S(1)} %get-tuple-element.33.e.refs_1_, f32[1024,128]{1,0:T(8,128)S(1)} %get-tuple-element.34.stat.refs_2_, bf16[1024,256]{1,0:T(8,128)(2,1)S(1)} %get-tuple-element.40.key, ...), custom_call_target="tpu_custom_call" | custom-call | flops 2000000000 | tf_op jit(solution)/shard_map/pallas_call | solution.py:485
  58.1 5.2 %shard_map.118 = (f32[1024,1]{1,0:T(8,128)S(1)}, bf16[4,256,128]{2,1,0:T(8,128)(2,1)S(1)}, bf16[4,256,128]{2,1,0:T(8,128)(2,1)S(1)}) custom-call(s32[8]{0:T(128)S(1)} %pad_add_fusion.table.refs_0_, f32[1,1024]{1,0:T(1,128)S(1)} %get-tuple-element.37.refs_1_, f32[1,1024]{1,0:T(1,128)S(1)} %collective-permute-done.6.refs_2_, ...), custom_call_target="tpu_custom_call" | custom-call | flops 2000000000 | tf_op jit(solution)/shard_map/pallas_call | solution.py:496
  63.4 2.2 %collective-permute-start.15 = (bf16[4,256,128]{2,1,0:T(8,128)(2,1)S(1)}, bf16[4,256,128]{2,1,0:T(8,128)(2,1)S(1)}, u32[]{:S(2)}, u32[]{:S(2)}) collective-permute-start(bf16[4,256,128]{2,1,0:T(8,128)(2,1)S(1)} %get-tuple-element.45), channel_id=1, source_target_pairs={{0,4},{4,0},{8,12},{12,8},{16,20},{20,16},{24,28},{28,24},{1,5},{5... | collective-permute-start | bytes 786440 | tf_op jit(solution)/shard_map/ppermute | solution.py:508
  65.6 8.4 %shard_map.119 = (bf16[272,1024]{1,0:T(8,128)(2,1)S(1)}, bf16[4,272,128]{2,1,0:T(8,128)(2,1)S(1)}, bf16[4,272,128]{2,1,0:T(8,128)(2,1)S(1)}) custom-call(s32[8]{0:T(128)S(1)} %pad_add_fusion.table.refs_0_, bf16[4,1024,1024]{2,1,0:T(8,128)(2,1)S(1)} %get-tuple-element.33.e.refs_1_, f32[1024,128]{1,0:T(8,128)S(1)} %get-tuple-element.34.stat.refs_2_, ...), custom_call_target="tpu_custom_call" | custom-call | flops 4000000000 | tf_op jit(solution)/shard_map/pallas_call | solution.py:518
  74.0 0.1 collective-permute-start.16
  74.1 0.1 add_convert_fusion.1
  74.2 8.7 %collective-permute-done.16 = bf16[4,272,128]{2,1,0:T(8,128)(2,1)S(1)} collective-permute-done((bf16[4,272,128]{2,1,0:T(8,128)(2,1)S(1)}, bf16[4,272,128]{2,1,0:T(8,128)(2,1)S(1)}, u32[]{:S(2)}, u32[]{:S(2)}) %collective-permute-start.16) | collective-permute-done | bytes 278560 | tf_op jit(solution)/shard_map/ppermute | solution.py:508
  82.8 0.1 add_convert_fusion
  83.0 0.1 collective-permute-start.17
  83.0 0.7 fusion.11
  83.7 0.5 collective-permute-start.14
  84.2 1.0 collective-permute-start.13
  85.2 0.3 collective-permute-start.12
  85.6 5.2 %collective-permute-done.17 = bf16[2,528,128]{2,1,0:T(8,128)(2,1)S(1)} collective-permute-done((bf16[2,528,128]{2,1,0:T(8,128)(2,1)S(1)}, bf16[2,528,128]{2,1,0:T(8,128)(2,1)S(1)}, u32[]{:S(2)}, u32[]{:S(2)}) %collective-permute-start.17) | collective-permute-done | bytes 270368 | tf_op jit(solution)/shard_map/ppermute | solution.py:508
  90.8 0.1 fusion.2
  90.9 1.3 collective-permute-start.18
  92.1 0.7 fusion.9
  92.8 5.9 %collective-permute-done.18 = bf16[1,528,128]{2,1,0:T(8,128)(2,1)S(1)} collective-permute-done((bf16[1,528,128]{2,1,0:T(8,128)(2,1)S(1)}, bf16[1,528,128]{2,1,0:T(8,128)(2,1)S(1)}, u32[]{:S(2)}, u32[]{:S(2)}) %collective-permute-start.18) | collective-permute-done | bytes 135200 | tf_op jit(solution)/shard_map/ppermute | solution.py:508
  98.7 1.5 %collective-permute-start.10 = (bf16[272,256]{1,0:T(8,128)(2,1)S(1)}, bf16[272,256]{1,0:T(8,128)(2,1)S(1)}, u32[]{:S(2)}, u32[]{:S(2)}) collective-permute-start(bf16[272,256]{1,0:T(8,128)(2,1)S(1)} %get-tuple-element.50), channel_id=1, source_target_pairs={{0,2},{1,3},{2,0},{3,1},{4,6},{5,7},{6,4},{7,5},{8,10},{9,11},{10,... | collective-permute-start | bytes 417800 | tf_op jit(solution)/shard_map/ppermute | solution.py:386
  100.3 0.1 collective-permute-start.9
  100.4 0.6 collective-permute-start.20
  101.0 0.2 reduce.1
  101.2 0.0 copy-start.3
  101.2 2.6 %shard_map.120.refs_6_ = f32[256,1024]{1,0:T(8,128)S(1)} custom-call(s32[8]{0:T(128)S(1)} %pad_add_fusion.table.refs_0_, bf16[256,256]{1,0:T(8,128)(2,1)S(1)} %get-tuple-element.58.refs_0_, bf16[256,256]{1,0:T(8,128)(2,1)S(1)} %collective-permute-done.12.refs_1_, bf16[256,256]{1,0:T(8,128)(2,1)S(1)} %collective-permute-done.13.refs_2_, ...), custom_call_target="tpu_custom_call" | custom-call | flops 1000000000 | tf_op jit(solution)/shard_map/pallas_call | solution.py:555
  103.9 0.2 collective-permute-start.19
  104.1 2.6 %collective-permute-done.20 = bf16[528,128]{1,0:T(8,128)(2,1)S(1)} collective-permute-done((bf16[528,128]{1,0:T(8,128)(2,1)S(1)}, bf16[528,128]{1,0:T(8,128)(2,1)S(1)}, u32[]{:S(2)}, u32[]{:S(2)}) %collective-permute-start.20) | collective-permute-done | bytes 135200 | tf_op jit(solution)/shard_map/ppermute | solution.py:386
  106.7 4.4 %shard_map.121 = bf16[8,32,1024]{2,1,0:T(8,128)(2,1)} custom-call(s32[8]{0:T(128)S(1)} %pad_add_fusion.table.refs_0_, bf16[272,256]{1,0:T(8,128)(2,1)S(1)} %get-tuple-element.52.refs_1_, bf16[272,256]{1,0:T(8,128)(2,1)S(1)} %collective-permute-done.9.refs_2_, bf16[272,256]{1,0:T(8,128)(2,1)S(1)} %collective-permute-done.10.refs_3_, ...), custom_call_target="tpu_custom_call" | custom-call | flops 1000000000 | tf_op jit(solution)/shard_map/pallas_call | solution.py:564
  111.1 3.8 %all-to-all-start.1 = ((bf16[8,32,1024]{2,1,0:T(8,128)(2,1)}), bf16[8,32,1024]{2,1,0:T(8,128)(2,1)S(1)}, u32[]{:S(2)}, u32[]{:S(2)}) async-start(bf16[8,32,1024]{2,1,0:T(8,128)(2,1)} %shard_map.121), calls=%async_computation.1 | async-start | bytes 1048576 | tf_op jit(solution)/shard_map/all_to_all | solution.py:389
  115.0 0.1 pad_maximum_fusion.1
  115.0 0.7 gather_fusion.1
  115.7 0.2 fusion.1
  115.9 0.0 copy-start.7
  116.0 0.1 pad_maximum_fusion
  116.0 0.7 dynamic-slice_bitcast_fusion
  116.7 13.3 %all-to-all-done.1 = bf16[8,32,1024]{2,1,0:T(8,128)(2,1)S(1)} async-done(((bf16[8,32,1024]{2,1,0:T(8,128)(2,1)}), bf16[8,32,1024]{2,1,0:T(8,128)(2,1)S(1)}, u32[]{:S(2)}, u32[]{:S(2)}) %all-to-all-start.1) | async-done | bytes 524320 | tf_op jit(solution)/shard_map/all_to_all | solution.py:389
  130.1 3.6 %all-to-all-start.2 = ((bf16[8,96,128]{2,1,0:T(8,128)(2,1)}), bf16[8,96,128]{2,1,0:T(8,128)(2,1)S(1)}, u32[]{:S(2)}, u32[]{:S(2)}) async-start(bf16[8,96,128]{2,1,0:T(8,128)(2,1)} %dynamic-slice_bitcast_fusion), calls=%async_computation.2 | async-start | bytes 393216 | tf_op jit(solution)/shard_map/all_to_all | solution.py:389
  133.7 0.1 dynamic_slice.13
  133.8 0.7 broadcast_multiply_fusion
  134.6 1.4 gather_fusion
  135.9 5.9 %all-to-all-done.2 = bf16[8,96,128]{2,1,0:T(8,128)(2,1)S(1)} async-done(((bf16[8,96,128]{2,1,0:T(8,128)(2,1)}), bf16[8,96,128]{2,1,0:T(8,128)(2,1)S(1)}, u32[]{:S(2)}, u32[]{:S(2)}) %all-to-all-start.2) | async-done | bytes 196640 | tf_op jit(solution)/shard_map/all_to_all | solution.py:389
  141.9 0.8 copy_bitcast_fusion
  (44 shorter events, 0.2 us)
Async XLA Ops:
  0.6 9.5 %copy-start = (s32[8,3]{0,1:T(4,128)S(1)}, s32[8,3]{0,1:T(4,128)}, u32[]{:S(2)}) copy-start(s32[8,3]{0,1:T(4,128)} %param.13) | copy-start | bytes 292
  0.6 9.8 %copy-start.4 = (f32[1024]{0:T(1024)S(1)}, f32[1024]{0:T(1024)}, u32[]{:S(2)}) copy-start(f32[1024]{0:T(1024)} %param.17) | copy-start | bytes 12292
  0.7 9.8 %copy-start.1 = (bf16[1024,1024]{1,0:T(8,128)(2,1)S(1)}, bf16[1024,1024]{1,0:T(8,128)(2,1)}, u32[]{:S(2)}) copy-start(bf16[1024,1024]{1,0:T(8,128)(2,1)} %w_out.1) | copy-start | bytes 6291460
  2.8 23.2 %all-to-all-start = ((bf16[8,32,1152]{2,1,0:T(8,128)(2,1)}), bf16[8,32,1152]{2,1,0:T(8,128)(2,1)S(1)}, u32[]{:S(2)}, u32[]{:S(2)}) async-start(bf16[8,32,1152]{2,1,0:T(8,128)(2,1)} %shard_map.112), calls=%async_computation | async-start | bytes 1179648 | tf_op jit(solution)/shard_map/all_to_all | solution.py:389
  10.5 15.5 %copy-start.5 = (f32[1024]{0:T(1024)S(1)}, f32[1024]{0:T(1024)}, u32[]{:S(2)}) copy-start(f32[1024]{0:T(1024)} %param.14) | copy-start | bytes 12292
  10.5 15.5 %copy-start.6 = (s32[1,8]{1,0:T(1,128)S(1)}, s32[1,8]{1,0:T(1,128)}, u32[]{:S(2)}) copy-start(s32[1,8]{1,0:T(1,128)} %refs_8_.1) | copy-start | bytes 100
  13.4 0.7 copy-start.2
  26.8 12.3 %collective-permute-start.1 = (bf16[256,1024]{1,0:T(8,128)(2,1)S(1)}, bf16[256,1024]{1,0:T(8,128)(2,1)S(1)}, u32[]{:S(2)}, u32[]{:S(2)}) collective-permute-start(bf16[256,1024]{1,0:T(8,128)(2,1)S(1)} %bitcast.59), channel_id=1, source_target_pairs={{0,2},{1,3},{2,0},{3,1},{4,6},{5,7},{6,4},{7,5},{8,10},{9,11},{10,... | collective-permute-start | bytes 1572872 | tf_op jit(solution)/shard_map/ppermute | solution.py:386
  28.4 12.9 %collective-permute-start = (bf16[256,1024]{1,0:T(8,128)(2,1)S(1)}, bf16[256,1024]{1,0:T(8,128)(2,1)S(1)}, u32[]{:S(2)}, u32[]{:S(2)}) collective-permute-start(bf16[256,1024]{1,0:T(8,128)(2,1)S(1)} %bitcast.60), channel_id=1, source_target_pairs={{0,1},{1,0},{2,3},{3,2},{4,5},{5,4},{6,7},{7,6},{8,9},{9,8},{10,11... | collective-permute-start | bytes 1572872 | tf_op jit(solution)/shard_map/ppermute | solution.py:386
  39.1 5.3 %collective-permute-start.2 = (bf16[256,1024]{1,0:T(8,128)(2,1)S(1)}, bf16[256,1024]{1,0:T(8,128)(2,1)S(1)}, u32[]{:S(2)}, u32[]{:S(2)}) collective-permute-start(bf16[256,1024]{1,0:T(8,128)(2,1)S(1)} %collective-permute-done.1.refs_3_), channel_id=1, source_target_pairs={{0,1},{1,0},{2,3},{3,2},{4,5},{5,4},{6,7},{7,6},{8,9},{9,8},{10,11... | collective-permute-start | bytes 1572872 | tf_op jit(solution)/shard_map/ppermute | solution.py:386
  39.1 5.0 %collective-permute-start.5 = (f32[8,256]{1,0:T(8,128)S(1)}, f32[8,256]{1,0:T(8,128)S(1)}, u32[]{:S(2)}, u32[]{:S(2)}) collective-permute-start(f32[8,256]{1,0:T(8,128)S(1)} %get-tuple-element.28.refs_5_), channel_id=1, source_target_pairs={{0,3},{1,2},{2,1},{3,0},{4,7},{5,6},{6,5},{7,4},{8,11},{9,10},{10,... | collective-permute-start | bytes 24584 | tf_op jit(solution)/shard_map/ppermute | solution.py:386
  40.8 3.7 %collective-permute-start.4 = (f32[8,256]{1,0:T(8,128)S(1)}, f32[8,256]{1,0:T(8,128)S(1)}, u32[]{:S(2)}, u32[]{:S(2)}) collective-permute-start(f32[8,256]{1,0:T(8,128)S(1)} %get-tuple-element.28.refs_5_), channel_id=1, source_target_pairs={{0,2},{1,3},{2,0},{3,1},{4,6},{5,7},{6,4},{7,5},{8,10},{9,11},{10,... | collective-permute-start | bytes 24584 | tf_op jit(solution)/shard_map/ppermute | solution.py:386
  41.3 3.1 %collective-permute-start.3 = (f32[8,256]{1,0:T(8,128)S(1)}, f32[8,256]{1,0:T(8,128)S(1)}, u32[]{:S(2)}, u32[]{:S(2)}) collective-permute-start(f32[8,256]{1,0:T(8,128)S(1)} %get-tuple-element.28.refs_5_), channel_id=1, source_target_pairs={{0,1},{1,0},{2,3},{3,2},{4,5},{5,4},{6,7},{7,6},{8,9},{9,8},{10,11... | collective-permute-start | bytes 24584 | tf_op jit(solution)/shard_map/ppermute | solution.py:386
  51.9 6.2 %collective-permute-start.8 = (f32[1,1024]{1,0:T(1,128)S(1)}, f32[1,1024]{1,0:T(1,128)S(1)}, u32[]{:S(2)}, u32[]{:S(2)}) collective-permute-start(f32[1,1024]{1,0:T(1,128)S(1)} %get-tuple-element.37.refs_1_), channel_id=1, source_target_pairs={{0,3},{1,2},{2,1},{3,0},{4,7},{5,6},{6,5},{7,4},{8,11},{9,10},{10,... | collective-permute-start | bytes 12296 | tf_op jit(solution)/shard_map/ppermute | solution.py:386
  53.4 4.8 %collective-permute-start.7 = (f32[1,1024]{1,0:T(1,128)S(1)}, f32[1,1024]{1,0:T(1,128)S(1)}, u32[]{:S(2)}, u32[]{:S(2)}) collective-permute-start(f32[1,1024]{1,0:T(1,128)S(1)} %get-tuple-element.37.refs_1_), channel_id=1, source_target_pairs={{0,2},{1,3},{2,0},{3,1},{4,6},{5,7},{6,4},{7,5},{8,10},{9,11},{10,... | collective-permute-start | bytes 12296 | tf_op jit(solution)/shard_map/ppermute | solution.py:386
  53.9 4.3 %collective-permute-start.6 = (f32[1,1024]{1,0:T(1,128)S(1)}, f32[1,1024]{1,0:T(1,128)S(1)}, u32[]{:S(2)}, u32[]{:S(2)}) collective-permute-start(f32[1,1024]{1,0:T(1,128)S(1)} %get-tuple-element.37.refs_1_), channel_id=1, source_target_pairs={{0,1},{1,0},{2,3},{3,2},{4,5},{5,4},{6,7},{7,6},{8,9},{9,8},{10,11... | collective-permute-start | bytes 12296 | tf_op jit(solution)/shard_map/ppermute | solution.py:386
  63.4 10.7 %collective-permute-start.15 = (bf16[4,256,128]{2,1,0:T(8,128)(2,1)S(1)}, bf16[4,256,128]{2,1,0:T(8,128)(2,1)S(1)}, u32[]{:S(2)}, u32[]{:S(2)}) collective-permute-start(bf16[4,256,128]{2,1,0:T(8,128)(2,1)S(1)} %get-tuple-element.45), channel_id=1, source_target_pairs={{0,4},{4,0},{8,12},{12,8},{16,20},{20,16},{24,28},{28,24},{1,5},{5... | collective-permute-start | bytes 786440 | tf_op jit(solution)/shard_map/ppermute | solution.py:508
  74.0 8.9 %collective-permute-start.16 = (bf16[4,272,128]{2,1,0:T(8,128)(2,1)S(1)}, bf16[4,272,128]{2,1,0:T(8,128)(2,1)S(1)}, u32[]{:S(2)}, u32[]{:S(2)}) collective-permute-start(bf16[4,272,128]{2,1,0:T(8,128)(2,1)S(1)} %get-tuple-element.47), channel_id=1, source_target_pairs={{0,4},{4,0},{8,12},{12,8},{16,20},{20,16},{24,28},{28,24},{1,5},{5... | collective-permute-start | bytes 835592 | tf_op jit(solution)/shard_map/ppermute | solution.py:508
  83.0 7.8 %collective-permute-start.17 = (bf16[2,528,128]{2,1,0:T(8,128)(2,1)S(1)}, bf16[2,528,128]{2,1,0:T(8,128)(2,1)S(1)}, u32[]{:S(2)}, u32[]{:S(2)}) collective-permute-start(bf16[2,528,128]{2,1,0:T(8,128)(2,1)S(1)} %fusion.5), channel_id=1, source_target_pairs={{0,8},{4,12},{8,0},{12,4},{16,24},{20,28},{24,16},{28,20},{1,9},{5... | collective-permute-start | bytes 811016 | tf_op jit(solution)/shard_map/ppermute | solution.py:508
  83.7 16.6 %collective-permute-start.14 = (bf16[256,256]{1,0:T(8,128)(2,1)S(1)}, bf16[256,256]{1,0:T(8,128)(2,1)S(1)}, u32[]{:S(2)}, u32[]{:S(2)}) collective-permute-start(bf16[256,256]{1,0:T(8,128)(2,1)S(1)} %get-tuple-element.55), channel_id=1, source_target_pairs={{0,3},{1,2},{2,1},{3,0},{4,7},{5,6},{6,5},{7,4},{8,11},{9,10},{10,... | collective-permute-start | bytes 393224 | tf_op jit(solution)/shard_map/ppermute | solution.py:386
  84.2 16.2 %collective-permute-start.13 = (bf16[256,256]{1,0:T(8,128)(2,1)S(1)}, bf16[256,256]{1,0:T(8,128)(2,1)S(1)}, u32[]{:S(2)}, u32[]{:S(2)}) collective-permute-start(bf16[256,256]{1,0:T(8,128)(2,1)S(1)} %get-tuple-element.56), channel_id=1, source_target_pairs={{0,2},{1,3},{2,0},{3,1},{4,6},{5,7},{6,4},{7,5},{8,10},{9,11},{10,... | collective-permute-start | bytes 393224 | tf_op jit(solution)/shard_map/ppermute | solution.py:386
  85.2 16.0 %collective-permute-start.12 = (bf16[256,256]{1,0:T(8,128)(2,1)}, bf16[256,256]{1,0:T(8,128)(2,1)S(1)}, u32[]{:S(2)}, u32[]{:S(2)}) collective-permute-start(bf16[256,256]{1,0:T(8,128)(2,1)} %get-tuple-element.57), channel_id=1, source_target_pairs={{0,1},{1,0},{2,3},{3,2},{4,5},{5,4},{6,7},{7,6},{8,9},{9,8},{10,11... | collective-permute-start | bytes 393224 | tf_op jit(solution)/shard_map/ppermute | solution.py:386
  90.9 7.9 %collective-permute-start.18 = (bf16[1,528,128]{2,1,0:T(8,128)(2,1)S(1)}, bf16[1,528,128]{2,1,0:T(8,128)(2,1)S(1)}, u32[]{:S(2)}, u32[]{:S(2)}) collective-permute-start(bf16[1,528,128]{2,1,0:T(8,128)(2,1)S(1)} %slice_bitcast_fusion), channel_id=1, source_target_pairs={{0,16},{4,20},{8,24},{12,28},{16,0},{20,4},{24,8},{28,12},{1,17},{... | collective-permute-start | bytes 405512 | tf_op jit(solution)/shard_map/ppermute | solution.py:508
  92.8 13.9 %collective-permute-start.11 = (bf16[272,256]{1,0:T(8,128)(2,1)}, bf16[272,256]{1,0:T(8,128)(2,1)S(1)}, u32[]{:S(2)}, u32[]{:S(2)}) collective-permute-start(bf16[272,256]{1,0:T(8,128)(2,1)} %get-tuple-element.49), channel_id=1, source_target_pairs={{0,3},{1,2},{2,1},{3,0},{4,7},{5,6},{6,5},{7,4},{8,11},{9,10},{10,... | collective-permute-start | bytes 417800 | tf_op jit(solution)/shard_map/ppermute | solution.py:386
  98.7 8.0 %collective-permute-start.10 = (bf16[272,256]{1,0:T(8,128)(2,1)S(1)}, bf16[272,256]{1,0:T(8,128)(2,1)S(1)}, u32[]{:S(2)}, u32[]{:S(2)}) collective-permute-start(bf16[272,256]{1,0:T(8,128)(2,1)S(1)} %get-tuple-element.50), channel_id=1, source_target_pairs={{0,2},{1,3},{2,0},{3,1},{4,6},{5,7},{6,4},{7,5},{8,10},{9,11},{10,... | collective-permute-start | bytes 417800 | tf_op jit(solution)/shard_map/ppermute | solution.py:386
  100.3 6.4 %collective-permute-start.9 = (bf16[272,256]{1,0:T(8,128)(2,1)S(1)}, bf16[272,256]{1,0:T(8,128)(2,1)S(1)}, u32[]{:S(2)}, u32[]{:S(2)}) collective-permute-start(bf16[272,256]{1,0:T(8,128)(2,1)S(1)} %get-tuple-element.51), channel_id=1, source_target_pairs={{0,1},{1,0},{2,3},{3,2},{4,5},{5,4},{6,7},{7,6},{8,9},{9,8},{10,11... | collective-permute-start | bytes 417800 | tf_op jit(solution)/shard_map/ppermute | solution.py:386
  100.4 6.3 %collective-permute-start.20 = (bf16[528,128]{1,0:T(8,128)(2,1)S(1)}, bf16[528,128]{1,0:T(8,128)(2,1)S(1)}, u32[]{:S(2)}, u32[]{:S(2)}) collective-permute-start(bf16[528,128]{1,0:T(8,128)(2,1)S(1)} %bitcast.76), channel_id=1, source_target_pairs={{0,2},{1,3},{2,0},{3,1},{4,6},{5,7},{6,4},{7,5},{8,10},{9,11},{10,... | collective-permute-start | bytes 405512 | tf_op jit(solution)/shard_map/ppermute | solution.py:386
  101.2 5.5 %copy-start.3 = (bf16[48,1024]{1,0:T(8,128)(2,1)S(1)}, bf16[48,1024]{1,0:T(8,128)(2,1)}, u32[]{:S(2)}) copy-start(bf16[48,1024]{1,0:T(8,128)(2,1)} %copy-done.2) | copy-start | bytes 294916
  103.9 11.1 %collective-permute-start.19 = (bf16[528,128]{1,0:T(8,128)(2,1)S(1)}, bf16[528,128]{1,0:T(8,128)(2,1)S(1)}, u32[]{:S(2)}, u32[]{:S(2)}) collective-permute-start(bf16[528,128]{1,0:T(8,128)(2,1)S(1)} %bitcast.77), channel_id=1, source_target_pairs={{0,1},{1,0},{2,3},{3,2},{4,5},{5,4},{6,7},{7,6},{8,9},{9,8},{10,11... | collective-permute-start | bytes 405512 | tf_op jit(solution)/shard_map/ppermute | solution.py:386
  106.7 8.3 %collective-permute-start.21 = (bf16[528,128]{1,0:T(8,128)(2,1)S(1)}, bf16[528,128]{1,0:T(8,128)(2,1)S(1)}, u32[]{:S(2)}, u32[]{:S(2)}) collective-permute-start(bf16[528,128]{1,0:T(8,128)(2,1)S(1)} %collective-permute-done.20), channel_id=1, source_target_pairs={{0,1},{1,0},{2,3},{3,2},{4,5},{5,4},{6,7},{7,6},{8,9},{9,8},{10,11... | collective-permute-start | bytes 405512 | tf_op jit(solution)/shard_map/ppermute | solution.py:386
  111.1 19.0 %all-to-all-start.1 = ((bf16[8,32,1024]{2,1,0:T(8,128)(2,1)}), bf16[8,32,1024]{2,1,0:T(8,128)(2,1)S(1)}, u32[]{:S(2)}, u32[]{:S(2)}) async-start(bf16[8,32,1024]{2,1,0:T(8,128)(2,1)} %shard_map.121), calls=%async_computation.1 | async-start | bytes 1048576 | tf_op jit(solution)/shard_map/all_to_all | solution.py:389
  115.9 17.8 %copy-start.7 = (s32[1,8]{1,0:T(1,128)S(1)}, s32[1,8]{1,0:T(1,128)}, u32[]{:S(2)}) copy-start(s32[1,8]{1,0:T(1,128)} %dest.1) | copy-start | bytes 100
  130.1 11.8 %all-to-all-start.2 = ((bf16[8,96,128]{2,1,0:T(8,128)(2,1)}), bf16[8,96,128]{2,1,0:T(8,128)(2,1)S(1)}, u32[]{:S(2)}, u32[]{:S(2)}) async-start(bf16[8,96,128]{2,1,0:T(8,128)(2,1)} %dynamic-slice_bitcast_fusion), calls=%async_computation.2 | async-start | bytes 393216 | tf_op jit(solution)/shard_map/all_to_all | solution.py:389
where the time goes:
time: 143 us
  waiting for transfers between devices  64.6 us (45%)
  Pallas kernels  41 us (29%)
  starting transfers between devices  28.3 us (20%)
  local copies, waits for them, and re-layouts  5.14 us (4%)
  other arithmetic  2.63 us (2%)
    all_to_all x3, waiting for transfers between devices, across(): lax.all_to_all(values, 'wide', split_axis=0, concat_axis=0, tiled=True)  31.1 us
    ppermute x4, waiting for transfers between devices, to_partner(): return lax.ppermute(values, 'wide', [(i, i ^ step) for i in range(wide)])  19.8 us
    all_to_all x3, starting transfers between devices, across(): lax.all_to_all(values, 'wide', split_axis=0, concat_axis=0, tiled=True)  14.7 us
    ppermute x18, waiting for transfers between devices, swap(): return lax.ppermute(values, 'narrow', [(i, i ^ m) for i in range(narrow)])  13.7 us
    ppermute x18, starting transfers between devices, swap(): return lax.ppermute(values, 'narrow', [(i, i ^ m) for i in range(narrow)])  9.92 us
    pallas_call x1, Pallas kernels, body(): indexed(lambda *refs: key_kernel(*refs, at_wide=narrow + lists), (shape(l...  8.38 us
    pallas_call x1, Pallas kernels, body(): indexed(lambda *refs: forward_kernel(*refs, narrow=narrow, lists=lists),...  7.47 us
    pallas_call x1, Pallas kernels, body(): indexed(lambda *refs: score_kernel(*refs, narrow=narrow, lists=lists), (s...  5.22 us
  transfers between devices with their start and end apart: 25, of which 9 were waited for; matrix products, arithmetic and copies ran while one was open for 4% of the time, Pallas kernels for 18%

commit v1 on v0

--- a/solution.py
+++ b/solution.py
@@ -220,7 +220,6 @@
     partials = refs[:narrow]
     given, x, a, grad_out, keep_out, send_out, lines, acc = refs[narrow:]
     local, _ = a.shape
-    width = x.shape[1]
     scale = (LANES // 2) ** -0.5
     pairs, _, chunk = keep_out.shape
     step = pl.program_id(0)
@@ -249,7 +248,7 @@
     grad = loss_scale * pulls / norm
     grad_out[...] = grad
     query = (a[...].astype(f32) * (grad * scale)).astype(bf16)
-    acc[...] += contract(query, x[:, :width], ((0,), (0,)))
+    acc[...] += contract(query, x[at, :], ((0,), (0,)))
 
     @pl.when(step == pl.num_programs(0) - 1)
     def _():
@@ -257,7 +256,7 @@
         halves(cut, pairs, table[narrow + lists], keep_out, send_out)
 
 
-def key_kernel(table, e, stat, query, z, grad, w_v, x_hbm, keys_out, keep_out, send_out, x, key_acc, c_acc, sem, at_wide):
+def key_kernel(table, e, stat, query, z, grad, w_v, x, keys_out, keep_out, send_out, key_acc, c_acc, at_wide):
     heads, total, _ = e.shape
     rows = query.shape[0]
     half = LANES // 2
@@ -265,11 +264,9 @@
     width = w_v.shape[0]
     pairs, lines, chunk = keep_out.shape
     step = pl.program_id(0)
-    copy = pltpu.make_async_copy(x_hbm, x, sem)
 
     @pl.when(step == 0)
     def _():
-        copy.start()
         key_acc[...] = jnp.zeros_like(key_acc)
         c_acc[...] = jnp.zeros_like(c_acc)
 
@@ -288,7 +285,6 @@
 
     @pl.when(step == pl.num_programs(0) - 1)
     def _():
-        copy.wait()
         c = c_acc[...]
         high = c.astype(bf16).astype(f32)
         parts = jnp.concatenate([high[:heads], (c - high)[:heads]], axis=0)
@@ -496,13 +492,13 @@
     grad, keep_q, send_q = indexed(
         lambda *refs: score_kernel(*refs, narrow=narrow, lists=lists),
         (shape(total, 1),) + (shape(wide // 2, own, chunk, dtype=bf16),) * 2,
-        [whole((1, total))] + [vmem()] * (narrow - 1) + [whole((8, total)), row_block(width), row_block(own)],
+        [whole((1, total))] + [vmem()] * (narrow - 1) + [whole((8, total)), vmem(), row_block(own)],
         (row_block(1),) + (whole((wide // 2, own, chunk)),) * 2,
         (narrow,),
         [pltpu.VMEM((8, total), f32), pltpu.VMEM((own, width), f32)],
         work=2 * 10**9,
         room=14,
-    )(table, partials[0], *map(near, partials[1:]), lines, x, a)
+    )(table, partials[0], *map(near, partials[1:]), lines, near(x), a)
 
     def to_partner(values, step):
         return lax.ppermute(values, "wide", [(i, i ^ step) for i in range(wide)])
@@ -525,19 +521,17 @@
             whole((HEADS, total)),
             row_block(1),
             pl.BlockSpec((width, own), lambda i, t: (0, 2 * narrow + t[0])),
-            pl.BlockSpec(memory_space=pl.ANY),
+            vmem(),
         ],
         (whole((lines_c, total)),) + (whole((wide // 2, lines_k, chunk)),) * 2,
         (narrow,),
         [
-            pltpu.VMEM((total, width), bf16),
             pltpu.VMEM((own, total), f32),
             pltpu.VMEM((8, total), f32),
-            pltpu.SemaphoreType.DMA,
         ],
         work=4 * 10**9,
         room=22,
-    )(table, near(e), stat, queries, z, grad, stay(w_qkv), x)
+    )(table, near(e), stat, queries, z, grad, stay(w_qkv), near(x))
 
     k_rows = [keys[:, :local]]
     k_rows += [swap(keys[:, m * local : (m + 1) * local], m) for m in range(1, narrow)]

time: 143 us -> 143 us (level)
  no operation moved by 1% of the time
where the time goes in v1:
time: 143 us
  waiting for transfers between devices  64.6 us (45%)
  Pallas kernels  40.9 us (29%)
  starting transfers between devices  28.3 us (20%)
  local copies, waits for them, and re-layouts  5.14 us (4%)
  other arithmetic  2.63 us (2%)
    all_to_all x3, waiting for transfers between devices, across(): lax.all_to_all(values, 'wide', split_axis=0, concat_axis=0, tiled=True)  31.1 us
    ppermute x4, waiting for transfers between devices, to_partner(): return lax.ppermute(values, 'wide', [(i, i ^ step) for i in range(wide)])  19.8 us
    all_to_all x3, starting transfers between devices, across(): lax.all_to_all(values, 'wide', split_axis=0, concat_axis=0, tiled=True)  14.7 us
    ppermute x18, waiting for transfers between devices, swap(): return lax.ppermute(values, 'narrow', [(i, i ^ m) for i in range(narrow)])  13.7 us
    ppermute x18, starting transfers between devices, swap(): return lax.ppermute(values, 'narrow', [(i, i ^ m) for i in range(narrow)])  9.92 us
    pallas_call x1, Pallas kernels, body(): indexed(lambda *refs: key_kernel(*refs, at_wide=narrow + lists), (shape(l...  8.29 us
    pallas_call x1, Pallas kernels, body(): indexed(lambda *refs: forward_kernel(*refs, narrow=narrow, lists=lists),...  7.47 us
    pallas_call x1, Pallas kernels, body(): indexed(lambda *refs: score_kernel(*refs, narrow=narrow, lists=lists), (s...  5.22 us
  transfers between devices with their start and end apart: 25, of which 9 were waited for; matrix products, arithmetic and copies ran while one was open for 4% of the time, Pallas kernels for 18%

profile of v1, /device:TPU:0, one launch (start us, length us, event | category | flops | bytes accessed | tf_op | source)
XLA Modules:
  0.0 142.6 jit_solution(2705397002137812167)
XLA Ops:
  0.6 0.0 copy-start
  0.7 2.1 %shard_map.112 = bf16[8,32,1152]{2,1,0:T(8,128)(2,1)} custom-call(s32[1,8]{1,0:T(1,128)} %dest.1, bf16[8,32,1024]{2,1,0:T(8,128)(2,1)} %bitcast.78, s32[1,256]{1,0:T(1,128)} %bitcast.85), custom_call_target="tpu_custom_call" | custom-call | tf_op jit(solution)/shard_map/pallas_call | solution.py:402
  2.8 7.3 %all-to-all-start = ((bf16[8,32,1152]{2,1,0:T(8,128)(2,1)}), bf16[8,32,1152]{2,1,0:T(8,128)(2,1)S(1)}, u32[]{:S(2)}, u32[]{:S(2)}) async-start(bf16[8,32,1152]{2,1,0:T(8,128)(2,1)} %shard_map.112), calls=%async_computation | async-start | bytes 1179648 | tf_op jit(solution)/shard_map/all_to_all | solution.py:385
  10.1 0.2 dynamic-slice_reduce_fusion
  10.3 0.2 reduce-window.9
  10.5 0.0 copy-start.6
  10.5 2.9 %shard_map.113 = (f32[1024,1]{1,0:T(8,128)S(1)}, bf16[48,1024]{1,0:T(8,128)(2,1)S(1)}, bf16[1024,128]{1,0:T(8,128)(2,1)S(1)}) custom-call(bf16[1024,3072]{1,0:T(8,128)(2,1)} %refs_5_.1, bf16[1024,1024]{1,0:T(8,128)(2,1)S(1)} %copy-done.1, f32[1,1024]{1,0:T(1,128)S(1)} %bitcast.63), custom_call_target="tpu_custom_call" | custom-call | flops 1000000000 | tf_op jit(solution)/shard_map/pallas_call | solution.py:407
  13.4 0.7 copy-done.2
  14.0 0.1 pad_add_fusion.table.refs_0_
  14.1 11.9 %all-to-all-done.incoming.refs_9_ = bf16[8,32,1152]{2,1,0:T(8,128)(2,1)S(1)} async-done(((bf16[8,32,1152]{2,1,0:T(8,128)(2,1)}), bf16[8,32,1152]{2,1,0:T(8,128)(2,1)S(1)}, u32[]{:S(2)}, u32[]{:S(2)}) %all-to-all-start) | async-done | bytes 589856 | tf_op jit(solution)/shard_map/all_to_all | solution.py:385
  26.0 0.9 shard_map.114
  26.8 1.6 %collective-permute-start.1 = (bf16[256,1024]{1,0:T(8,128)(2,1)S(1)}, bf16[256,1024]{1,0:T(8,128)(2,1)S(1)}, u32[]{:S(2)}, u32[]{:S(2)}) collective-permute-start(bf16[256,1024]{1,0:T(8,128)(2,1)S(1)} %bitcast.59), channel_id=1, source_target_pairs={{0,2},{1,3},{2,0},{3,1},{4,6},{5,7},{6,4},{7,5},{8,10},{9,11},{10,... | collective-permute-start | bytes 1572872 | tf_op jit(solution)/shard_map/ppermute | solution.py:382
  28.4 10.7 %collective-permute-done.1.refs_3_ = bf16[256,1024]{1,0:T(8,128)(2,1)S(1)} collective-permute-done((bf16[256,1024]{1,0:T(8,128)(2,1)S(1)}, bf16[256,1024]{1,0:T(8,128)(2,1)S(1)}, u32[]{:S(2)}, u32[]{:S(2)}) %collective-permute-start.1) | collective-permute-done | bytes 524320 | tf_op jit(solution)/shard_map/ppermute | solution.py:382
  39.1 0.0 collective-permute-start.2
  39.1 1.6 %collective-permute-start.5 = (f32[8,256]{1,0:T(8,128)S(1)}, f32[8,256]{1,0:T(8,128)S(1)}, u32[]{:S(2)}, u32[]{:S(2)}) collective-permute-start(f32[8,256]{1,0:T(8,128)S(1)} %get-tuple-element.28.refs_5_), channel_id=1, source_target_pairs={{0,3},{1,2},{2,1},{3,0},{4,7},{5,6},{6,5},{7,4},{8,11},{9,10},{10,... | collective-permute-start | bytes 24584 | tf_op jit(solution)/shard_map/ppermute | solution.py:382
  40.8 0.5 collective-permute-start.4
  41.3 2.8 %shard_map.115 = (bf16[1024,512]{1,0:T(8,128)(2,1)S(1)}, bf16[512,256]{1,0:T(8,128)(2,1)S(1)}, bf16[512,256]{1,0:T(8,128)(2,1)S(1)}, f32[16,512]{1,0:T(8,128)S(1)}) custom-call(s32[8]{0:T(128)S(1)} %pad_add_fusion.table.refs_0_, bf16[256,1024]{1,0:T(8,128)(2,1)S(1)} %bitcast.61, bf16[256,1024]{1,0:T(8,128)(2,1)S(1)} %collective-permute-done.second.refs_2_, ...), custom_call_target="tpu_custom_call" | custom-call | flops 1000000000 | tf_op jit(solution)/shard_map/pallas_call | solution.py:427
  44.1 0.0 collective-permute-done.5.refs_8_
  44.1 0.3 collective-permute-done.4.refs_7_
  44.4 0.0 collective-permute-done.3.refs_6_
  44.4 7.5 %shard_map.116 = (bf16[1024,256]{1,0:T(8,128)(2,1)S(1)}, bf16[4,1024,1024]{2,1,0:T(8,128)(2,1)S(1)}, bf16[1024,256]{1,0:T(8,128)(2,1)S(1)}, bf16[1024,1024]{1,0:...) custom-call(s32[8]{0:T(128)S(1)} %pad_add_fusion.table.refs_0_, ...), custom_call_target="tpu_custom_call" | custom-call | flops 4000000000 | tf_op jit(solution)/shard_map/pallas_call | solution.py:447
  51.9 1.5 %collective-permute-start.8 = (f32[1,1024]{1,0:T(1,128)S(1)}, f32[1,1024]{1,0:T(1,128)S(1)}, u32[]{:S(2)}, u32[]{:S(2)}) collective-permute-start(f32[1,1024]{1,0:T(1,128)S(1)} %get-tuple-element.37.refs_1_), channel_id=1, source_target_pairs={{0,3},{1,2},{2,1},{3,0},{4,7},{5,6},{6,5},{7,4},{8,11},{9,10},{10,... | collective-permute-start | bytes 12296 | tf_op jit(solution)/shard_map/ppermute | solution.py:382
  53.4 0.5 collective-permute-start.7
  53.9 4.2 %shard_map.117.refs_7_ = bf16[1024,256]{1,0:T(8,128)(2,1)S(1)} custom-call(s32[8]{0:T(128)S(1)} %pad_add_fusion.table.refs_0_, bf16[4,1024,1024]{2,1,0:T(8,128)(2,1)S(1)} %get-tuple-element.33.e.refs_1_, f32[1024,128]{1,0:T(8,128)S(1)} %get-tuple-element.34.stat.refs_2_, bf16[1024,256]{1,0:T(8,128)(2,1)S(1)} %get-tuple-element.40.key, ...), custom_call_target="tpu_custom_call" | custom-call | flops 2000000000 | tf_op jit(solution)/shard_map/pallas_call | solution.py:481
  58.1 5.2 %shard_map.118 = (f32[1024,1]{1,0:T(8,128)S(1)}, bf16[4,256,128]{2,1,0:T(8,128)(2,1)S(1)}, bf16[4,256,128]{2,1,0:T(8,128)(2,1)S(1)}) custom-call(s32[8]{0:T(128)S(1)} %pad_add_fusion.table.refs_0_, f32[1,1024]{1,0:T(1,128)S(1)} %get-tuple-element.37.refs_1_, f32[1,1024]{1,0:T(1,128)S(1)} %collective-permute-done.6.refs_2_, ...), custom_call_target="tpu_custom_call" | custom-call | flops 2000000000 | tf_op jit(solution)/shard_map/pallas_call | solution.py:492
  63.4 2.2 %collective-permute-start.15 = (bf16[4,256,128]{2,1,0:T(8,128)(2,1)S(1)}, bf16[4,256,128]{2,1,0:T(8,128)(2,1)S(1)}, u32[]{:S(2)}, u32[]{:S(2)}) collective-permute-start(bf16[4,256,128]{2,1,0:T(8,128)(2,1)S(1)} %get-tuple-element.45), channel_id=1, source_target_pairs={{0,4},{4,0},{8,12},{12,8},{16,20},{20,16},{24,28},{28,24},{1,5},{5... | collective-permute-start | bytes 786440 | tf_op jit(solution)/shard_map/ppermute | solution.py:504
  65.6 8.3 %shard_map.119 = (bf16[272,1024]{1,0:T(8,128)(2,1)S(1)}, bf16[4,272,128]{2,1,0:T(8,128)(2,1)S(1)}, bf16[4,272,128]{2,1,0:T(8,128)(2,1)S(1)}) custom-call(s32[8]{0:T(128)S(1)} %pad_add_fusion.table.refs_0_, bf16[4,1024,1024]{2,1,0:T(8,128)(2,1)S(1)} %get-tuple-element.33.e.refs_1_, f32[1024,128]{1,0:T(8,128)S(1)} %get-tuple-element.34.stat.refs_2_, ...), custom_call_target="tpu_custom_call" | custom-call | flops 4000000000 | tf_op jit(solution)/shard_map/pallas_call | solution.py:514
  73.9 0.1 collective-permute-start.16
  74.0 0.1 add_convert_fusion.1
  74.1 8.7 %collective-permute-done.16 = bf16[4,272,128]{2,1,0:T(8,128)(2,1)S(1)} collective-permute-done((bf16[4,272,128]{2,1,0:T(8,128)(2,1)S(1)}, bf16[4,272,128]{2,1,0:T(8,128)(2,1)S(1)}, u32[]{:S(2)}, u32[]{:S(2)}) %collective-permute-start.16) | collective-permute-done | bytes 278560 | tf_op jit(solution)/shard_map/ppermute | solution.py:504
  82.8 0.1 add_convert_fusion
  82.9 0.1 collective-permute-start.17
  82.9 0.7 fusion.11
  83.6 0.5 collective-permute-start.14
  84.1 1.0 collective-permute-start.13
  85.2 0.3 collective-permute-start.12
  85.5 5.2 %collective-permute-done.17 = bf16[2,528,128]{2,1,0:T(8,128)(2,1)S(1)} collective-permute-done((bf16[2,528,128]{2,1,0:T(8,128)(2,1)S(1)}, bf16[2,528,128]{2,1,0:T(8,128)(2,1)S(1)}, u32[]{:S(2)}, u32[]{:S(2)}) %collective-permute-start.17) | collective-permute-done | bytes 270368 | tf_op jit(solution)/shard_map/ppermute | solution.py:504
  90.7 0.1 fusion.2
  90.8 1.3 collective-permute-start.18
  92.0 0.7 fusion.9
  92.7 5.9 %collective-permute-done.18 = bf16[1,528,128]{2,1,0:T(8,128)(2,1)S(1)} collective-permute-done((bf16[1,528,128]{2,1,0:T(8,128)(2,1)S(1)}, bf16[1,528,128]{2,1,0:T(8,128)(2,1)S(1)}, u32[]{:S(2)}, u32[]{:S(2)}) %collective-permute-start.18) | collective-permute-done | bytes 135200 | tf_op jit(solution)/shard_map/ppermute | solution.py:504
  98.6 1.5 %collective-permute-start.10 = (bf16[272,256]{1,0:T(8,128)(2,1)S(1)}, bf16[272,256]{1,0:T(8,128)(2,1)S(1)}, u32[]{:S(2)}, u32[]{:S(2)}) collective-permute-start(bf16[272,256]{1,0:T(8,128)(2,1)S(1)} %get-tuple-element.50), channel_id=1, source_target_pairs={{0,2},{1,3},{2,0},{3,1},{4,6},{5,7},{6,4},{7,5},{8,10},{9,11},{10,... | collective-permute-start | bytes 417800 | tf_op jit(solution)/shard_map/ppermute | solution.py:382
  100.2 0.1 collective-permute-start.9
  100.3 0.6 collective-permute-start.20
  100.9 0.2 reduce.1
  101.1 0.0 copy-start.3
  101.1 2.6 %shard_map.120.refs_6_ = f32[256,1024]{1,0:T(8,128)S(1)} custom-call(s32[8]{0:T(128)S(1)} %pad_add_fusion.table.refs_0_, bf16[256,256]{1,0:T(8,128)(2,1)S(1)} %get-tuple-element.58.refs_0_, bf16[256,256]{1,0:T(8,128)(2,1)S(1)} %collective-permute-done.12.refs_1_, bf16[256,256]{1,0:T(8,128)(2,1)S(1)} %collective-permute-done.13.refs_2_, ...), custom_call_target="tpu_custom_call" | custom-call | flops 1000000000 | tf_op jit(solution)/shard_map/pallas_call | solution.py:549
  103.8 0.2 collective-permute-start.19
  104.0 2.6 %collective-permute-done.20 = bf16[528,128]{1,0:T(8,128)(2,1)S(1)} collective-permute-done((bf16[528,128]{1,0:T(8,128)(2,1)S(1)}, bf16[528,128]{1,0:T(8,128)(2,1)S(1)}, u32[]{:S(2)}, u32[]{:S(2)}) %collective-permute-start.20) | collective-permute-done | bytes 135200 | tf_op jit(solution)/shard_map/ppermute | solution.py:382
  106.6 4.4 %shard_map.121 = bf16[8,32,1024]{2,1,0:T(8,128)(2,1)} custom-call(s32[8]{0:T(128)S(1)} %pad_add_fusion.table.refs_0_, bf16[272,256]{1,0:T(8,128)(2,1)S(1)} %get-tuple-element.52.refs_1_, bf16[272,256]{1,0:T(8,128)(2,1)S(1)} %collective-permute-done.9.refs_2_, bf16[272,256]{1,0:T(8,128)(2,1)S(1)} %collective-permute-done.10.refs_3_, ...), custom_call_target="tpu_custom_call" | custom-call | flops 1000000000 | tf_op jit(solution)/shard_map/pallas_call | solution.py:558
  111.0 3.8 %all-to-all-start.1 = ((bf16[8,32,1024]{2,1,0:T(8,128)(2,1)}), bf16[8,32,1024]{2,1,0:T(8,128)(2,1)S(1)}, u32[]{:S(2)}, u32[]{:S(2)}) async-start(bf16[8,32,1024]{2,1,0:T(8,128)(2,1)} %shard_map.121), calls=%async_computation.1 | async-start | bytes 1048576 | tf_op jit(solution)/shard_map/all_to_all | solution.py:385
  114.9 0.1 pad_maximum_fusion.1
  114.9 0.7 gather_fusion.1
  115.6 0.2 fusion.1
  115.8 0.0 copy-start.7
  115.9 0.1 pad_maximum_fusion
  115.9 0.7 dynamic-slice_bitcast_fusion
  116.6 13.3 %all-to-all-done.1 = bf16[8,32,1024]{2,1,0:T(8,128)(2,1)S(1)} async-done(((bf16[8,32,1024]{2,1,0:T(8,128)(2,1)}), bf16[8,32,1024]{2,1,0:T(8,128)(2,1)S(1)}, u32[]{:S(2)}, u32[]{:S(2)}) %all-to-all-start.1) | async-done | bytes 524320 | tf_op jit(solution)/shard_map/all_to_all | solution.py:385
  130.0 3.6 %all-to-all-start.2 = ((bf16[8,96,128]{2,1,0:T(8,128)(2,1)}), bf16[8,96,128]{2,1,0:T(8,128)(2,1)S(1)}, u32[]{:S(2)}, u32[]{:S(2)}) async-start(bf16[8,96,128]{2,1,0:T(8,128)(2,1)} %dynamic-slice_bitcast_fusion), calls=%async_computation.2 | async-start | bytes 393216 | tf_op jit(solution)/shard_map/all_to_all | solution.py:385
  133.6 0.1 dynamic_slice.13
  133.7 0.7 broadcast_multiply_fusion
  134.5 1.4 gather_fusion
  135.8 5.9 %all-to-all-done.2 = bf16[8,96,128]{2,1,0:T(8,128)(2,1)S(1)} async-done(((bf16[8,96,128]{2,1,0:T(8,128)(2,1)}), bf16[8,96,128]{2,1,0:T(8,128)(2,1)S(1)}, u32[]{:S(2)}, u32[]{:S(2)}) %all-to-all-start.2) | async-done | bytes 196640 | tf_op jit(solution)/shard_map/all_to_all | solution.py:385
  141.8 0.8 copy_bitcast_fusion
  (44 shorter events, 0.2 us)
Async XLA Ops:
  0.6 9.5 %copy-start = (s32[8,3]{0,1:T(4,128)S(1)}, s32[8,3]{0,1:T(4,128)}, u32[]{:S(2)}) copy-start(s32[8,3]{0,1:T(4,128)} %param.13) | copy-start | bytes 292
  0.6 9.8 %copy-start.4 = (f32[1024]{0:T(1024)S(1)}, f32[1024]{0:T(1024)}, u32[]{:S(2)}) copy-start(f32[1024]{0:T(1024)} %param.17) | copy-start | bytes 12292
  0.7 9.8 %copy-start.1 = (bf16[1024,1024]{1,0:T(8,128)(2,1)S(1)}, bf16[1024,1024]{1,0:T(8,128)(2,1)}, u32[]{:S(2)}) copy-start(bf16[1024,1024]{1,0:T(8,128)(2,1)} %w_out.1) | copy-start | bytes 6291460
  2.8 23.2 %all-to-all-start = ((bf16[8,32,1152]{2,1,0:T(8,128)(2,1)}), bf16[8,32,1152]{2,1,0:T(8,128)(2,1)S(1)}, u32[]{:S(2)}, u32[]{:S(2)}) async-start(bf16[8,32,1152]{2,1,0:T(8,128)(2,1)} %shard_map.112), calls=%async_computation | async-start | bytes 1179648 | tf_op jit(solution)/shard_map/all_to_all | solution.py:385
  10.5 15.5 %copy-start.5 = (f32[1024]{0:T(1024)S(1)}, f32[1024]{0:T(1024)}, u32[]{:S(2)}) copy-start(f32[1024]{0:T(1024)} %param.14) | copy-start | bytes 12292
  10.5 15.5 %copy-start.6 = (s32[1,8]{1,0:T(1,128)S(1)}, s32[1,8]{1,0:T(1,128)}, u32[]{:S(2)}) copy-start(s32[1,8]{1,0:T(1,128)} %refs_8_.1) | copy-start | bytes 100
  13.4 0.7 copy-start.2
  26.8 12.3 %collective-permute-start.1 = (bf16[256,1024]{1,0:T(8,128)(2,1)S(1)}, bf16[256,1024]{1,0:T(8,128)(2,1)S(1)}, u32[]{:S(2)}, u32[]{:S(2)}) collective-permute-start(bf16[256,1024]{1,0:T(8,128)(2,1)S(1)} %bitcast.59), channel_id=1, source_target_pairs={{0,2},{1,3},{2,0},{3,1},{4,6},{5,7},{6,4},{7,5},{8,10},{9,11},{10,... | collective-permute-start | bytes 1572872 | tf_op jit(solution)/shard_map/ppermute | solution.py:382
  28.4 12.9 %collective-permute-start = (bf16[256,1024]{1,0:T(8,128)(2,1)S(1)}, bf16[256,1024]{1,0:T(8,128)(2,1)S(1)}, u32[]{:S(2)}, u32[]{:S(2)}) collective-permute-start(bf16[256,1024]{1,0:T(8,128)(2,1)S(1)} %bitcast.60), channel_id=1, source_target_pairs={{0,1},{1,0},{2,3},{3,2},{4,5},{5,4},{6,7},{7,6},{8,9},{9,8},{10,11... | collective-permute-start | bytes 1572872 | tf_op jit(solution)/shard_map/ppermute | solution.py:382
  39.1 5.3 %collective-permute-start.2 = (bf16[256,1024]{1,0:T(8,128)(2,1)S(1)}, bf16[256,1024]{1,0:T(8,128)(2,1)S(1)}, u32[]{:S(2)}, u32[]{:S(2)}) collective-permute-start(bf16[256,1024]{1,0:T(8,128)(2,1)S(1)} %collective-permute-done.1.refs_3_), channel_id=1, source_target_pairs={{0,1},{1,0},{2,3},{3,2},{4,5},{5,4},{6,7},{7,6},{8,9},{9,8},{10,11... | collective-permute-start | bytes 1572872 | tf_op jit(solution)/shard_map/ppermute | solution.py:382
  39.1 5.0 %collective-permute-start.5 = (f32[8,256]{1,0:T(8,128)S(1)}, f32[8,256]{1,0:T(8,128)S(1)}, u32[]{:S(2)}, u32[]{:S(2)}) collective-permute-start(f32[8,256]{1,0:T(8,128)S(1)} %get-tuple-element.28.refs_5_), channel_id=1, source_target_pairs={{0,3},{1,2},{2,1},{3,0},{4,7},{5,6},{6,5},{7,4},{8,11},{9,10},{10,... | collective-permute-start | bytes 24584 | tf_op jit(solution)/shard_map/ppermute | solution.py:382
  40.8 3.7 %collective-permute-start.4 = (f32[8,256]{1,0:T(8,128)S(1)}, f32[8,256]{1,0:T(8,128)S(1)}, u32[]{:S(2)}, u32[]{:S(2)}) collective-permute-start(f32[8,256]{1,0:T(8,128)S(1)} %get-tuple-element.28.refs_5_), channel_id=1, source_target_pairs={{0,2},{1,3},{2,0},{3,1},{4,6},{5,7},{6,4},{7,5},{8,10},{9,11},{10,... | collective-permute-start | bytes 24584 | tf_op jit(solution)/shard_map/ppermute | solution.py:382
  41.3 3.1 %collective-permute-start.3 = (f32[8,256]{1,0:T(8,128)S(1)}, f32[8,256]{1,0:T(8,128)S(1)}, u32[]{:S(2)}, u32[]{:S(2)}) collective-permute-start(f32[8,256]{1,0:T(8,128)S(1)} %get-tuple-element.28.refs_5_), channel_id=1, source_target_pairs={{0,1},{1,0},{2,3},{3,2},{4,5},{5,4},{6,7},{7,6},{8,9},{9,8},{10,11... | collective-permute-start | bytes 24584 | tf_op jit(solution)/shard_map/ppermute | solution.py:382
  51.9 6.2 %collective-permute-start.8 = (f32[1,1024]{1,0:T(1,128)S(1)}, f32[1,1024]{1,0:T(1,128)S(1)}, u32[]{:S(2)}, u32[]{:S(2)}) collective-permute-start(f32[1,1024]{1,0:T(1,128)S(1)} %get-tuple-element.37.refs_1_), channel_id=1, source_target_pairs={{0,3},{1,2},{2,1},{3,0},{4,7},{5,6},{6,5},{7,4},{8,11},{9,10},{10,... | collective-permute-start | bytes 12296 | tf_op jit(solution)/shard_map/ppermute | solution.py:382
  53.4 4.8 %collective-permute-start.7 = (f32[1,1024]{1,0:T(1,128)S(1)}, f32[1,1024]{1,0:T(1,128)S(1)}, u32[]{:S(2)}, u32[]{:S(2)}) collective-permute-start(f32[1,1024]{1,0:T(1,128)S(1)} %get-tuple-element.37.refs_1_), channel_id=1, source_target_pairs={{0,2},{1,3},{2,0},{3,1},{4,6},{5,7},{6,4},{7,5},{8,10},{9,11},{10,... | collective-permute-start | bytes 12296 | tf_op jit(solution)/shard_map/ppermute | solution.py:382
  53.9 4.3 %collective-permute-start.6 = (f32[1,1024]{1,0:T(1,128)S(1)}, f32[1,1024]{1,0:T(1,128)S(1)}, u32[]{:S(2)}, u32[]{:S(2)}) collective-permute-start(f32[1,1024]{1,0:T(1,128)S(1)} %get-tuple-element.37.refs_1_), channel_id=1, source_target_pairs={{0,1},{1,0},{2,3},{3,2},{4,5},{5,4},{6,7},{7,6},{8,9},{9,8},{10,11... | collective-permute-start | bytes 12296 | tf_op jit(solution)/shard_map/ppermute | solution.py:382
  63.4 10.6 %collective-permute-start.15 = (bf16[4,256,128]{2,1,0:T(8,128)(2,1)S(1)}, bf16[4,256,128]{2,1,0:T(8,128)(2,1)S(1)}, u32[]{:S(2)}, u32[]{:S(2)}) collective-permute-start(bf16[4,256,128]{2,1,0:T(8,128)(2,1)S(1)} %get-tuple-element.45), channel_id=1, source_target_pairs={{0,4},{4,0},{8,12},{12,8},{16,20},{20,16},{24,28},{28,24},{1,5},{5... | collective-permute-start | bytes 786440 | tf_op jit(solution)/shard_map/ppermute | solution.py:504
  73.9 8.9 %collective-permute-start.16 = (bf16[4,272,128]{2,1,0:T(8,128)(2,1)S(1)}, bf16[4,272,128]{2,1,0:T(8,128)(2,1)S(1)}, u32[]{:S(2)}, u32[]{:S(2)}) collective-permute-start(bf16[4,272,128]{2,1,0:T(8,128)(2,1)S(1)} %get-tuple-element.47), channel_id=1, source_target_pairs={{0,4},{4,0},{8,12},{12,8},{16,20},{20,16},{24,28},{28,24},{1,5},{5... | collective-permute-start | bytes 835592 | tf_op jit(solution)/shard_map/ppermute | solution.py:504
  82.9 7.8 %collective-permute-start.17 = (bf16[2,528,128]{2,1,0:T(8,128)(2,1)S(1)}, bf16[2,528,128]{2,1,0:T(8,128)(2,1)S(1)}, u32[]{:S(2)}, u32[]{:S(2)}) collective-permute-start(bf16[2,528,128]{2,1,0:T(8,128)(2,1)S(1)} %fusion.5), channel_id=1, source_target_pairs={{0,8},{4,12},{8,0},{12,4},{16,24},{20,28},{24,16},{28,20},{1,9},{5... | collective-permute-start | bytes 811016 | tf_op jit(solution)/shard_map/ppermute | solution.py:504
  83.6 16.6 %collective-permute-start.14 = (bf16[256,256]{1,0:T(8,128)(2,1)S(1)}, bf16[256,256]{1,0:T(8,128)(2,1)S(1)}, u32[]{:S(2)}, u32[]{:S(2)}) collective-permute-start(bf16[256,256]{1,0:T(8,128)(2,1)S(1)} %get-tuple-element.55), channel_id=1, source_target_pairs={{0,3},{1,2},{2,1},{3,0},{4,7},{5,6},{6,5},{7,4},{8,11},{9,10},{10,... | collective-permute-start | bytes 393224 | tf_op jit(solution)/shard_map/ppermute | solution.py:382
  84.1 16.2 %collective-permute-start.13 = (bf16[256,256]{1,0:T(8,128)(2,1)S(1)}, bf16[256,256]{1,0:T(8,128)(2,1)S(1)}, u32[]{:S(2)}, u32[]{:S(2)}) collective-permute-start(bf16[256,256]{1,0:T(8,128)(2,1)S(1)} %get-tuple-element.56), channel_id=1, source_target_pairs={{0,2},{1,3},{2,0},{3,1},{4,6},{5,7},{6,4},{7,5},{8,10},{9,11},{10,... | collective-permute-start | bytes 393224 | tf_op jit(solution)/shard_map/ppermute | solution.py:382
  85.2 16.0 %collective-permute-start.12 = (bf16[256,256]{1,0:T(8,128)(2,1)}, bf16[256,256]{1,0:T(8,128)(2,1)S(1)}, u32[]{:S(2)}, u32[]{:S(2)}) collective-permute-start(bf16[256,256]{1,0:T(8,128)(2,1)} %get-tuple-element.57), channel_id=1, source_target_pairs={{0,1},{1,0},{2,3},{3,2},{4,5},{5,4},{6,7},{7,6},{8,9},{9,8},{10,11... | collective-permute-start | bytes 393224 | tf_op jit(solution)/shard_map/ppermute | solution.py:382
  90.8 7.9 %collective-permute-start.18 = (bf16[1,528,128]{2,1,0:T(8,128)(2,1)S(1)}, bf16[1,528,128]{2,1,0:T(8,128)(2,1)S(1)}, u32[]{:S(2)}, u32[]{:S(2)}) collective-permute-start(bf16[1,528,128]{2,1,0:T(8,128)(2,1)S(1)} %slice_bitcast_fusion), channel_id=1, source_target_pairs={{0,16},{4,20},{8,24},{12,28},{16,0},{20,4},{24,8},{28,12},{1,17},{... | collective-permute-start | bytes 405512 | tf_op jit(solution)/shard_map/ppermute | solution.py:504
  92.7 13.9 %collective-permute-start.11 = (bf16[272,256]{1,0:T(8,128)(2,1)}, bf16[272,256]{1,0:T(8,128)(2,1)S(1)}, u32[]{:S(2)}, u32[]{:S(2)}) collective-permute-start(bf16[272,256]{1,0:T(8,128)(2,1)} %get-tuple-element.49), channel_id=1, source_target_pairs={{0,3},{1,2},{2,1},{3,0},{4,7},{5,6},{6,5},{7,4},{8,11},{9,10},{10,... | collective-permute-start | bytes 417800 | tf_op jit(solution)/shard_map/ppermute | solution.py:382
  98.6 8.0 %collective-permute-start.10 = (bf16[272,256]{1,0:T(8,128)(2,1)S(1)}, bf16[272,256]{1,0:T(8,128)(2,1)S(1)}, u32[]{:S(2)}, u32[]{:S(2)}) collective-permute-start(bf16[272,256]{1,0:T(8,128)(2,1)S(1)} %get-tuple-element.50), channel_id=1, source_target_pairs={{0,2},{1,3},{2,0},{3,1},{4,6},{5,7},{6,4},{7,5},{8,10},{9,11},{10,... | collective-permute-start | bytes 417800 | tf_op jit(solution)/shard_map/ppermute | solution.py:382
  100.2 6.4 %collective-permute-start.9 = (bf16[272,256]{1,0:T(8,128)(2,1)S(1)}, bf16[272,256]{1,0:T(8,128)(2,1)S(1)}, u32[]{:S(2)}, u32[]{:S(2)}) collective-permute-start(bf16[272,256]{1,0:T(8,128)(2,1)S(1)} %get-tuple-element.51), channel_id=1, source_target_pairs={{0,1},{1,0},{2,3},{3,2},{4,5},{5,4},{6,7},{7,6},{8,9},{9,8},{10,11... | collective-permute-start | bytes 417800 | tf_op jit(solution)/shard_map/ppermute | solution.py:382
  100.3 6.3 %collective-permute-start.20 = (bf16[528,128]{1,0:T(8,128)(2,1)S(1)}, bf16[528,128]{1,0:T(8,128)(2,1)S(1)}, u32[]{:S(2)}, u32[]{:S(2)}) collective-permute-start(bf16[528,128]{1,0:T(8,128)(2,1)S(1)} %bitcast.76), channel_id=1, source_target_pairs={{0,2},{1,3},{2,0},{3,1},{4,6},{5,7},{6,4},{7,5},{8,10},{9,11},{10,... | collective-permute-start | bytes 405512 | tf_op jit(solution)/shard_map/ppermute | solution.py:382
  101.1 5.5 %copy-start.3 = (bf16[48,1024]{1,0:T(8,128)(2,1)S(1)}, bf16[48,1024]{1,0:T(8,128)(2,1)}, u32[]{:S(2)}) copy-start(bf16[48,1024]{1,0:T(8,128)(2,1)} %copy-done.2) | copy-start | bytes 294916
  103.8 11.1 %collective-permute-start.19 = (bf16[528,128]{1,0:T(8,128)(2,1)S(1)}, bf16[528,128]{1,0:T(8,128)(2,1)S(1)}, u32[]{:S(2)}, u32[]{:S(2)}) collective-permute-start(bf16[528,128]{1,0:T(8,128)(2,1)S(1)} %bitcast.77), channel_id=1, source_target_pairs={{0,1},{1,0},{2,3},{3,2},{4,5},{5,4},{6,7},{7,6},{8,9},{9,8},{10,11... | collective-permute-start | bytes 405512 | tf_op jit(solution)/shard_map/ppermute | solution.py:382
  106.6 8.2 %collective-permute-start.21 = (bf16[528,128]{1,0:T(8,128)(2,1)S(1)}, bf16[528,128]{1,0:T(8,128)(2,1)S(1)}, u32[]{:S(2)}, u32[]{:S(2)}) collective-permute-start(bf16[528,128]{1,0:T(8,128)(2,1)S(1)} %collective-permute-done.20), channel_id=1, source_target_pairs={{0,1},{1,0},{2,3},{3,2},{4,5},{5,4},{6,7},{7,6},{8,9},{9,8},{10,11... | collective-permute-start | bytes 405512 | tf_op jit(solution)/shard_map/ppermute | solution.py:382
  111.0 18.9 %all-to-all-start.1 = ((bf16[8,32,1024]{2,1,0:T(8,128)(2,1)}), bf16[8,32,1024]{2,1,0:T(8,128)(2,1)S(1)}, u32[]{:S(2)}, u32[]{:S(2)}) async-start(bf16[8,32,1024]{2,1,0:T(8,128)(2,1)} %shard_map.121), calls=%async_computation.1 | async-start | bytes 1048576 | tf_op jit(solution)/shard_map/all_to_all | solution.py:385
  115.8 17.8 %copy-start.7 = (s32[1,8]{1,0:T(1,128)S(1)}, s32[1,8]{1,0:T(1,128)}, u32[]{:S(2)}) copy-start(s32[1,8]{1,0:T(1,128)} %dest.1) | copy-start | bytes 100
  130.0 11.8 %all-to-all-start.2 = ((bf16[8,96,128]{2,1,0:T(8,128)(2,1)}), bf16[8,96,128]{2,1,0:T(8,128)(2,1)S(1)}, u32[]{:S(2)}, u32[]{:S(2)}) async-start(bf16[8,96,128]{2,1,0:T(8,128)(2,1)} %dynamic-slice_bitcast_fusion), calls=%async_computation.2 | async-start | bytes 393216 | tf_op jit(solution)/shard_map/all_to_all | solution.py:385
